TPU v7x, 128 devices: a whole 4x4x4 slice. The times are simulated.
128 devices in a mesh: samp: 4 (over y), band: 32 (over z, x, core).
Axes of the slice: x: 4, y: 4, z: 4, core: 2. Of those that a mesh axis runs over, the one named last changes fastest.
Arguments:
- tod: float32 [32, 16384], P('band', 'samp'), may hold values from -6 to 6
- cycle: int32 [32, 16384], P('band', 'samp'), may hold values from 0 to 3
- phi_cell: int32 [32, 16384], P('band', 'samp'), may hold values from 0 to 8191
- psi_bin: int32 [32, 16384], P('band', 'samp'), may hold values from 0 to 32
- offset: int32 [32, 16384], P('band', 'samp'), may hold values from 0 to 7
- counts: int32 [32, 4], P('band', 'samp'), may hold values from 1 to 4096, as said below
- kernel: float32 [8, 4], replicated, may hold values from 0.1 to 1
- wigner: float32 [32, 80, 33, 64, 128], P('band', 'samp'), may hold values from -0.015625 to 0.015625
- beam: float32 [64, 33], replicated, may hold values from -1 to 1
Outputs:
- sky: float32 [32, 80, 128], P('band', 'samp')
Inputs may be any that keep to these rules, and one draw needn't show every extreme that they name: counts[b, s] samples of shard s in band b are live, those at the first positions of the shard; some shard is full.
All inputs are finite; a program needn't handle non-finite values.
Results may differ from a plain program's by a relative error of at most 0.0025.
Values sent between devices are 32-bit elements; how exact they have to be, the bound alone decides.
No kernel may reach another device: no remote copies, remote signals or barrier semaphores. Data moves between devices by JAX's collectives and lax.ppermute only.
A program may use at most 128 MiB of HBM per device.

v0:
```python
import math

import jax
import jax.numpy as jnp
import numpy as np
from jax import lax
from jax.experimental import pallas as pl
from jax.experimental.pallas import tpu as pltpu
from jax.sharding import PartitionSpec as P

PHI = 8192
K = 33
M = 2560
LB = 64
S_DEV = 4096
RT = 128
PER_DEV = 20
ROWS = 32
BLOCK = 4
CELL_ROWS = 560
TILES = 11
BF = jnp.bfloat16


def split_host(x):
    x = np.asarray(x, np.float32)
    hi = x.astype(BF)
    lo = (x - hi.astype(np.float32)).astype(BF)
    return np.stack([hi, lo])


def host_tables():
    a = np.arange(16)
    cl = np.arange(16)
    ang = 2 * np.pi * ((a[:, None] * cl[None, :]) % 16) / 16
    fc, fs = np.cos(ang), -np.sin(ang)
    f_main = np.concatenate([np.repeat(fc, 32, 1), np.repeat(fs, 32, 1)], 1)
    f_last = np.zeros((128, 256))
    f_last[:16, :16] = fc
    f_last[:16, 128:144] = fs
    b = np.arange(512)
    m2 = (5 * np.arange(32)[None, :] + np.arange(5)[:, None]).reshape(-1)
    ang = 2 * np.pi * ((m2[:, None] * b[None, :]) % 512) / 512
    w_phi = np.concatenate([np.cos(ang), np.sin(ang)], 0)
    lanes = np.concatenate([np.arange(512) // 32, np.where(np.arange(128) < 16, np.arange(128), 0)])
    ang = 2 * np.pi * (16 * np.arange(33)[:, None] * lanes[None, :]) / PHI
    t_hi = np.stack([np.cos(ang), np.sin(ang)]).astype(np.float32)
    ang = 2 * np.pi * (np.arange(16)[:, None] * lanes[None, :]) / PHI
    t_lo = np.stack([np.cos(ang), np.sin(ang)]).astype(np.float32)
    k = np.arange(K)
    ang = 2 * np.pi * ((k[:, None] * k[None, :]) % K) / K
    d = np.zeros((80, 80))
    c, s = np.cos(ang), np.sin(ang)
    d[0:66:2, 0:32], d[0:66:2, 64] = c[:, :32], c[:, 32]
    d[0:66:2, 32:64], d[0:66:2, 65] = s[:, :32], s[:, 32]
    d[1:66:2, 0:32], d[1:66:2, 64] = -s[:, :32], -s[:, 32]
    d[1:66:2, 32:64], d[1:66:2, 65] = c[:, :32], c[:, 32]
    return split_host(f_main), split_host(f_last), split_host(w_phi), t_hi, t_lo, split_host(d)


F_MAIN, F_LAST, W_PHI, TW_HI, TW_LO, D_PSI = host_tables()


def split(x):
    hi = x.astype(BF)
    lo = (x - hi.astype(jnp.float32)).astype(BF)
    return hi, lo


def dot(x, y):
    return jnp.dot(x, y, preferred_element_type=jnp.float32)


def dot_nt(x, y):
    return lax.dot_general(x, y, (((1,), (1,)), ((), ())), preferred_element_type=jnp.float32)


def spectra_kernel(
    g_ref, kern_ref, mine_ref, fm_ref, fl_ref, w_ref, th_ref, tl_ref, out_ref,
    s_ref, acc_ref, lt_ref, rt_ref, s1_ref, last_ref, zh_ref, zl_ref,
):
    mine = mine_ref[0]
    slot = lax.broadcasted_iota(jnp.int32, (ROWS, 128), 0) * 128 + lax.broadcasted_iota(
        jnp.int32, (ROWS, 128), 1
    )
    for s in range(4):
        tod = g_ref[s, 0]
        phi = g_ref[s, 1].astype(jnp.int32)
        psi = g_ref[s, 2].astype(jnp.int32)
        off = g_ref[s, 3].astype(jnp.int32)
        cyc = g_ref[s, 4].astype(jnp.int32)
        cnt = g_ref[s, 5].astype(jnp.int32)
        live = (slot < cnt) & (cyc == mine)
        first = jnp.where(phi == 0, PHI - 1, phi - 1)
        b_hi = (first & 511) >> 4
        is_last = psi == 32
        at = pl.ds(s * ROWS, ROWS)
        s_ref[0, at, :] = jnp.where(live, jnp.where(is_last, b_hi, psi), -1).astype(jnp.float32)
        s_ref[1, at, :] = (first >> 9).astype(jnp.float32)
        s_ref[2, at, :] = jnp.where(is_last, 33, b_hi).astype(jnp.float32)
        s_ref[3, at, :] = (first & 15).astype(jnp.float32)
        for t in range(4):
            weight = jnp.zeros((ROWS, 128), jnp.float32)
            for o in range(8):
                weight = jnp.where(off == o, kern_ref[o, t], weight)
            s_ref[4 + t, at, :] = (tod * weight).astype(BF).astype(jnp.float32)

    acc_ref[...] = jnp.zeros_like(acc_ref)
    sub = lax.broadcasted_iota(jnp.int32, (16, 128), 0).astype(jnp.float32).astype(BF)
    zero = jnp.zeros((16, 128), BF)
    one = jnp.ones((16, 128), BF)

    def build(row0):
        for j in range(BLOCK):

            def row(ch):
                v = s_ref[ch, pl.ds(row0 + j, 1), :]
                return jnp.broadcast_to(v, (16, 128)).astype(BF)

            n_hi, n_lo, m_hi, m_lo = row(0), row(1), row(2), row(3)
            a0, a1, a2, a3 = row(4), row(5), row(6), row(7)
            ones = jnp.where(n_lo == sub, one, zero)
            d = sub - m_lo
            main = jnp.where(
                d == 0.0, a0, jnp.where(d == 1.0, a1, jnp.where(d == 2.0, a2, jnp.where(d == 3.0, a3, zero)))
            )
            spill = jnp.where(
                d == -15.0, a1, jnp.where(d == -14.0, a2, jnp.where(d == -13.0, a3, zero))
            )
            at = pl.ds(j * 128, 128)
            for h in range(32):
                lt_ref[h * 16 : (h + 1) * 16, at] = jnp.where(n_hi == float(h), ones, zero)
            before = None
            for h in range(35):
                here = m_hi == float(h)
                rest = zero if before is None else jnp.where(before, spill, zero)
                rt_ref[h * 16 : (h + 1) * 16, at] = jnp.where(here, main, rest)
                before = here

    def step(i, base):
        build(base + i * BLOCK)
        acc_ref[...] += dot_nt(rt_ref[...], lt_ref[...])
        return base

    for s in range(4):
        count = jnp.max(g_ref[s, 5, 0:8, :]).astype(jnp.int32)
        lax.fori_loop(0, (count + BLOCK * 128 - 1) // (BLOCK * 128), step, s * ROWS)

    lane = lax.broadcasted_iota(jnp.int32, (16, 1024), 1) & 31
    lane = lane.astype(jnp.float32).astype(BF)
    for q in range(32):
        keep = lane == float(q)
        for part in range(2):
            s1_ref[part, q * 16 : (q + 1) * 16, :] = jnp.where(
                keep, fm_ref[part], jnp.zeros((16, 1024), BF)
            )

    def chunk(r0, at):
        tile = acc_ref[r0 : r0 + 16, (at // 8) * 128 : (at // 8) * 128 + 128]
        shift = (at % 8) * 16
        return tile if shift == 0 else pltpu.roll(tile, 128 - shift, 1)

    for h in range(33):
        tile = jnp.zeros((16, 128), jnp.float32)
        if h < 32:
            tile = tile + chunk(528, h)
        if h > 0:
            tile = tile + chunk(544, h - 1)
        last_ref[h * 16 : (h + 1) * 16, :] = tile

    def first_stage(r0, rows):
        at = pl.ds(r0, rows)
        xh, xl = split(acc_ref[at, :])
        y = dot(xh, s1_ref[0]) + dot(xl, s1_ref[0]) + dot(xh, s1_ref[1])
        xh, xl = split(last_ref[at, :])
        y_last = dot(xh, fl_ref[0]) + dot(xl, fl_ref[0]) + dot(xh, fl_ref[1])
        out = []
        for i in range(rows // 16):
            h = r0 // 16 + i
            ch, sh = th_ref[0, h : h + 1, :], th_ref[1, h : h + 1, :]
            cw = ch * tl_ref[0] - sh * tl_ref[1]
            sw = sh * tl_ref[0] + ch * tl_ref[1]
            at = slice(i * 16, (i + 1) * 16)
            yr = jnp.concatenate([y[at, :512], y_last[at, :128]], 1)
            yi = jnp.concatenate([y[at, 512:], y_last[at, 128:]], 1)
            out.append((yr * cw + yi * sw, yi * cw - yr * sw))
        return out

    halo = first_stage(512, 16)[0]
    for r0 in range(0, 512, 128):
        for i, (zr, zi) in enumerate(first_stage(r0, 128)):
            if r0 == 0 and i == 0:
                zr, zi = zr + halo[0], zi + halo[1]
            rh, rl = split(zr)
            ih, il = split(zi)
            at = slice(r0 + i * 16, r0 + (i + 1) * 16)
            for g in range(5):
                take = slice(g * 128, (g + 1) * 128)
                zh_ref[at, g * 256 : g * 256 + 128] = rh[:, take]
                zh_ref[at, g * 256 + 128 : g * 256 + 256] = ih[:, take]
                zl_ref[at, g * 256 : g * 256 + 128] = rl[:, take]
                zl_ref[at, g * 256 + 128 : g * 256 + 256] = il[:, take]

    def put(s_to, tile_no, value):
        out_ref[pl.ds(s_to * TILES + tile_no, 32, stride=4 * TILES), :] = value

    for g in range(5):
        take = slice(g * 256, (g + 1) * 256)
        zh, zl = zh_ref[:, take], zl_ref[:, take]
        p = dot(w_ref[0], zh) + dot(w_ref[1], zh) + dot(w_ref[0], zl)
        parts = (p[:160, :128] + p[160:, 128:], p[:160, 128:] - p[160:, :128])
        if g < 4:
            for c in range(2):
                for e in range(5):
                    s_to, t = divmod(e * 4 + g, 5)
                    put(s_to, c * 5 + t, parts[c][e * 32 : (e + 1) * 32])
            continue
        lanes = lax.broadcasted_iota(jnp.int32, (32, 128), 1)
        for s_to in range(4):
            row = jnp.zeros((32, 128), jnp.float32)
            for c in range(2):
                j = 0
                while j < PER_DEV:
                    e, cl = divmod(PER_DEV * s_to + j, 16)
                    length = min(16 - cl, PER_DEV - j)
                    to = 64 * c + j
                    piece = parts[c][e * 32 : (e + 1) * 32]
                    shift = (to - cl) % 128
                    piece = piece if shift == 0 else pltpu.roll(piece, shift, 1)
                    row = jnp.where((lanes >= to) & (lanes < to + length), piece, row)
                    j += length
            put(s_to, 10, row)


def sky_kernel(r_ref, wig_ref, beam_ref, d_ref, out_ref, wbuf, gh_ref, gl_ref, h_ref, bb_ref, sems):
    def fetch(m):
        return pltpu.make_async_copy(wig_ref.at[m], wbuf.at[m], sems.at[m])

    for m in range(PER_DEV):
        fetch(m).start()

    for k in range(K):
        bb_ref[k] = jnp.broadcast_to(beam_ref[:, k : k + 1], (LB, 128))

    def tile(t):
        return r_ref[pl.ds(t, 128, stride=TILES), :].T

    rem = tile(10)
    sub = lax.broadcasted_iota(jnp.int32, (16, 128), 0)
    for t in range(5):
        planes = (tile(t), tile(5 + t))
        for jj in range(4):
            j = t * 4 + jj
            half = slice((j % 2) * 128, (j % 2) * 128 + 128)
            for c in range(2):
                hi, lo = split(planes[c][jj * 32 : (jj + 1) * 32])
                gh_ref[j // 2, c * 32 : (c + 1) * 32, half] = hi
                gl_ref[j // 2, c * 32 : (c + 1) * 32, half] = lo
            extra = jnp.where(sub == 0, rem[j : j + 1], jnp.where(sub == 1, rem[64 + j : 65 + j], 0.0))
            hi, lo = split(extra)
            gh_ref[j // 2, 64:80, half] = hi
            gl_ref[j // 2, 64:80, half] = lo
    for i in range(PER_DEV // 2):
        h = dot(d_ref[0], gh_ref[i]) + dot(d_ref[1], gh_ref[i]) + dot(d_ref[0], gl_ref[i])
        h_ref[2 * i] = h[:, :128]
        h_ref[2 * i + 1] = h[:, 128:]

    ones = jnp.ones((16, 128), BF)

    def order(m, carry):
        fetch(m).wait()
        real = [jnp.zeros((8, 128), jnp.float32)] * 8
        imag = [jnp.zeros((8, 128), jnp.float32)] * 8
        for k in range(K):
            hr = jnp.broadcast_to(h_ref[m, 2 * k : 2 * k + 1, :], (8, 128))
            hi = jnp.broadcast_to(h_ref[m, 2 * k + 1 : 2 * k + 2, :], (8, 128))
            for i in range(8):
                at = slice(i * 8, (i + 1) * 8)
                w = wbuf[m, k, at, :] * bb_ref[k, at, :]
                real[i] = real[i] + w * hr
                imag[i] = imag[i] + w * hi
        both = jnp.concatenate(real + imag, 0)
        hi, lo = split(both)
        tail = (both - hi.astype(jnp.float32) - lo.astype(jnp.float32)).astype(BF)
        res = dot_nt(ones, hi) + dot_nt(ones, lo) + dot_nt(ones, tail)
        out_ref[pl.ds(m, 1), :] = res[0:1]
        return carry

    lax.fori_loop(0, PER_DEV, order, 0)


def vmem():
    return pl.BlockSpec(memory_space=pltpu.VMEM)


def spectra(gathered, kernel, mine):
    return pl.pallas_call(
        spectra_kernel,
        out_shape=jax.ShapeDtypeStruct((128 * TILES, 128), jnp.float32),
        in_specs=[
            vmem(),
            pl.BlockSpec(memory_space=pltpu.SMEM),
            pl.BlockSpec(memory_space=pltpu.SMEM),
            vmem(), vmem(), vmem(), vmem(), vmem(),
        ],
        out_specs=vmem(),
        scratch_shapes=[
            pltpu.VMEM((8, 128, 128), jnp.float32),
            pltpu.VMEM((CELL_ROWS, 512), jnp.float32),
            pltpu.VMEM((512, BLOCK * 128), BF),
            pltpu.VMEM((CELL_ROWS, BLOCK * 128), BF),
            pltpu.VMEM((2, 512, 1024), BF),
            pltpu.VMEM((528, 128), jnp.float32),
            pltpu.VMEM((512, 1280), BF),
            pltpu.VMEM((512, 1280), BF),
        ],
        compiler_params=pltpu.CompilerParams(vmem_limit_bytes=32 << 20),
        name="spectra",
    )(gathered, kernel, mine, F_MAIN, F_LAST, W_PHI, TW_HI, TW_LO)


def sky_of(received, wigner, beam):
    return pl.pallas_call(
        sky_kernel,
        out_shape=jax.ShapeDtypeStruct((PER_DEV, 2 * LB), jnp.float32),
        in_specs=[vmem(), pl.BlockSpec(memory_space=pl.ANY), vmem(), vmem()],
        out_specs=vmem(),
        scratch_shapes=[
            pltpu.VMEM((PER_DEV, K, LB, RT), jnp.float32),
            pltpu.VMEM((PER_DEV // 2, 80, 256), BF),
            pltpu.VMEM((PER_DEV // 2, 80, 256), BF),
            pltpu.VMEM((PER_DEV, 80, 128), jnp.float32),
            pltpu.VMEM((K, LB, 128), jnp.float32),
            pltpu.SemaphoreType.DMA((PER_DEV,)),
        ],
        compiler_params=pltpu.CompilerParams(vmem_limit_bytes=40 << 20),
        name="sky",
    )(received, wigner, beam, D_PSI)


def body(tod, cycle, phi_cell, psi_bin, offset, counts, kernel, wigner, beam):
    rows = [
        x.reshape(ROWS, 128).astype(jnp.float32) for x in (tod, phi_cell, psi_bin, offset, cycle)
    ]
    rows.append(jnp.broadcast_to(counts.astype(jnp.float32), (ROWS, 128)))
    gathered = lax.all_gather(jnp.stack(rows), "samp")
    mine = lax.axis_index("samp").astype(jnp.int32).reshape(1)
    sent = spectra(gathered, kernel, mine)
    received = lax.all_to_all(
        sent.reshape(128, 1, TILES * 128), ("band", "samp"), 0, 0, tiled=True
    ).reshape(128 * TILES, 128)
    return sky_of(received, wigner[0], beam).reshape(1, PER_DEV, 2 * LB)


def solution(mesh):
    split_both = P("band", "samp")
    placed = (split_both,) * 6 + (P(), P("band", "samp", None, None, None), P())
    return jax.shard_map(
        body, mesh=mesh, in_specs=placed, out_specs=P("band", "samp", None), check_vma=False
    )
```

profile of v0, /device:TPU:1, one launch (start us, length us, event | category | flops | bytes accessed | tf_op | source)
XLA Modules:
  0.0 78.4 jit_solution(7167495583013957021)
XLA Ops:
  0.0 0.7 constant_dynamic-update-slice_fusion.5
  0.7 0.7 convert_element_type.55
  1.5 0.7 convert_element_type.57
  2.2 0.7 convert_element_type.59
  2.9 0.7 convert_element_type.61
  4.4 12.1 %all-gather = f32[24,32,128]{2,1,0:T(8,128)S(1)} all-gather(f32[6,32,128]{2,1,0:T(8,128)S(1)} %constant_dynamic-update-slice_fusion), channel_id=2, replica_groups=mesh['samp'=4,'band'=32] {'samp'}, dimensions={0}, use_global_device_ids=true | all-gather | bytes 491520 | tf_op jit(solution)/shard_map/all_gather | solution.py:346
  16.5 0.8 copy.19.kern_ref
  17.2 0.0 copy-start
  17.2 1.1 %copy-done = bf16[2,320,512]{2,1,0:T(8,128)(2,1)S(1)} copy-done((bf16[2,320,512]{2,1,0:T(8,128)(2,1)S(1)}, bf16[2,320,512]{2,1,0:T(8,128)(2,1)}, u32[]{:S(2)}) %copy-start) | copy-done | bytes 655384
  18.3 0.0 copy-start.1
  18.3 0.9 %copy-done.1 = f32[2,33,640]{2,1,0:T(8,128)S(1)} copy-done((f32[2,33,640]{2,1,0:T(8,128)S(1)}, f32[2,33,640]{2,1,0:T(8,128)}, u32[]{:S(2)}) %copy-start.1) | copy-done | bytes 168984
  19.3 0.0 copy-start.2
  19.3 0.9 %copy-done.2 = bf16[2,128,256]{2,1,0:T(8,128)(2,1)S(1)} copy-done((bf16[2,128,256]{2,1,0:T(8,128)(2,1)S(1)}, bf16[2,128,256]{2,1,0:T(8,128)(2,1)}, u32[]{:S(2)}) %copy-start.2) | copy-done | bytes 131096
  20.2 0.0 copy-start.3
  20.2 0.9 %copy-done.3 = f32[2,16,640]{2,1,0:T(8,128)S(1)} copy-done((f32[2,16,640]{2,1,0:T(8,128)S(1)}, f32[2,16,640]{2,1,0:T(8,128)}, u32[]{:S(2)}) %copy-start.3) | copy-done | bytes 81944
  21.1 0.0 copy-start.4
  21.1 0.8 %copy-done.4 = bf16[2,16,1024]{2,1,0:T(8,128)(2,1)S(1)} copy-done((bf16[2,16,1024]{2,1,0:T(8,128)(2,1)S(1)}, bf16[2,16,1024]{2,1,0:T(8,128)(2,1)}, u32[]{:S(2)}) %copy-start.4) | copy-done | bytes 65560
  21.9 15.9 %spectra.1 = f32[1408,128]{1,0:T(8,128)} custom-call(f32[4,6,32,128]{3,2,1,0:T(8,128)S(1)} %bitcast.13, f32[8,4]{1,0:T(8,128)S(1)} %copy.19.kern_ref, s32[1]{0:T(128)} %bitcast.7.mine_ref, bf16[2,16,1024]{2,1,0:T(8,128)(2,1)S(1)} %copy-done.4, bf16[2,128,256]{2,1,0:T(8,128)(2,1)S(1)} %copy-done.2, bf16[2,320,512]{2,1,0:T(8,128)(2,1)S(1)} %copy-done, ...), custom_call_target="tpu_custom_call" | custom-call | tf_op jit(solution)/shard_map/spectra/pallas_call | solution.py:297
  37.8 14.1 %all-to-all-start = ((f32[128,1,1408]{2,1,0:T(1,128)}), f32[128,1,1408]{2,1,0:T(1,128)S(1)}, u32[]{:S(2)}, u32[]{:S(2)}) async-start(f32[128,1,1408]{2,1,0:T(1,128)} %bitcast.8), calls=%async_computation | async-start | bytes 1441792 | tf_op jit(solution)/shard_map/all_to_all | solution.py:349
  51.8 0.8 %copy.21.beam_ref = f32[64,33]{1,0:T(8,128)S(1)} copy(f32[64,33]{0,1:T(8,128)} %param.23) | data formatting | bytes 16896 | tf_op args[8]
  52.7 15.0 %all-to-all-done = f32[128,1,1408]{2,1,0:T(1,128)S(1)} async-done(((f32[128,1,1408]{2,1,0:T(1,128)}), f32[128,1,1408]{2,1,0:T(1,128)S(1)}, u32[]{:S(2)}, u32[]{:S(2)}) %all-to-all-start) | async-done | bytes 720928 | tf_op jit(solution)/shard_map/all_to_all | solution.py:349
  67.7 0.0 copy-start.5
  67.7 0.8 copy-done.5
  68.5 9.4 %sky.1 = f32[20,128]{1,0:T(8,128)S(1)} custom-call(f32[1408,128]{1,0:T(8,128)S(1)} %bitcast.12, f32[20,33,64,128]{3,2,1,0:T(8,128)} %bitcast.15, f32[64,33]{1,0:T(8,128)S(1)} %copy.21.beam_ref, bf16[2,80,80]{2,1,0:T(8,128)(2,1)S(1)} %copy-done.5), custom_call_target="tpu_custom_call" | custom-call | tf_op jit(solution)/shard_map/sky/pallas_call | solution.py:323
  77.8 0.6 copy.22
  (5 shorter events, 0.0 us)
Async XLA Ops:
  17.2 1.1 %copy-start = (bf16[2,320,512]{2,1,0:T(8,128)(2,1)S(1)}, bf16[2,320,512]{2,1,0:T(8,128)(2,1)}, u32[]{:S(2)}) copy-start(bf16[2,320,512]{2,1,0:T(8,128)(2,1)} %constant.20.clone.w_ref) | copy-start | bytes 1966084
  18.3 0.9 %copy-start.1 = (f32[2,33,640]{2,1,0:T(8,128)S(1)}, f32[2,33,640]{2,1,0:T(8,128)}, u32[]{:S(2)}) copy-start(f32[2,33,640]{2,1,0:T(8,128)} %constant.21.clone.th_ref) | copy-start | bytes 506884
  19.3 0.9 %copy-start.2 = (bf16[2,128,256]{2,1,0:T(8,128)(2,1)S(1)}, bf16[2,128,256]{2,1,0:T(8,128)(2,1)}, u32[]{:S(2)}) copy-start(bf16[2,128,256]{2,1,0:T(8,128)(2,1)} %constant.19.clone.fl_ref) | copy-start | bytes 393220
  20.2 0.9 %copy-start.3 = (f32[2,16,640]{2,1,0:T(8,128)S(1)}, f32[2,16,640]{2,1,0:T(8,128)}, u32[]{:S(2)}) copy-start(f32[2,16,640]{2,1,0:T(8,128)} %constant.22.clone.tl_ref) | copy-start | bytes 245764
  21.1 0.8 %copy-start.4 = (bf16[2,16,1024]{2,1,0:T(8,128)(2,1)S(1)}, bf16[2,16,1024]{2,1,0:T(8,128)(2,1)}, u32[]{:S(2)}) copy-start(bf16[2,16,1024]{2,1,0:T(8,128)(2,1)} %constant.18.clone.fm_ref) | copy-start | bytes 196612
  37.8 29.9 %all-to-all-start = ((f32[128,1,1408]{2,1,0:T(1,128)}), f32[128,1,1408]{2,1,0:T(1,128)S(1)}, u32[]{:S(2)}, u32[]{:S(2)}) async-start(f32[128,1,1408]{2,1,0:T(1,128)} %bitcast.8), calls=%async_computation | async-start | bytes 1441792 | tf_op jit(solution)/shard_map/all_to_all | solution.py:349
  67.7 0.8 copy-start.5
where the time goes:
time: 77.7 us; the launch traced here: 78.4 us
  Pallas kernels  25.2 us (32%)
  waiting for transfers between devices  15 us (19%)
  starting transfers between devices  14.1 us (18%)
  blocking collectives  12.1 us (16%)
  local copies, waits for them, and re-layouts  8.34 us (11%)
  other arithmetic  2.93 us (4%)
    pallas_call x1, Pallas kernels, spectra(): pl.pallas_call(spectra_kernel, out_shape=jax.ShapeDtypeStruct((128 * TILE...  15.9 us
    all_to_all x1, waiting for transfers between devices, body(): lax.all_to_all(sent.reshape(128, 1, TILES * 128), ('band', 'samp'), 0, 0,...  15 us
    all_to_all x1, starting transfers between devices, body(): lax.all_to_all(sent.reshape(128, 1, TILES * 128), ('band', 'samp'), 0, 0,...  14.1 us
    all_gather x1, blocking collectives, body(): gathered = lax.all_gather(jnp.stack(rows), 'samp')  12.1 us
    pallas_call x1, Pallas kernels, sky_of(): pl.pallas_call(sky_kernel, out_shape=jax.ShapeDtypeStruct((PER_DEV, 2 * L...  9.36 us
    unnamed x19, local copies, waits for them, and re-layouts  7.72 us
    convert_element_type x4, other arithmetic, body(): x.reshape(ROWS, 128).astype(jnp.float32)  2.93 us
  transfers between devices with their start and end apart: 1, of which 1 were waited for; matrix products, arithmetic and copies ran while one was open for 1% of the time, Pallas kernels for 0%

commit v1 on v0

--- a/solution.py
+++ b/solution.py
@@ -1,5 +1,3 @@
-import math
-
 import jax
 import jax.numpy as jnp
 import numpy as np
@@ -8,11 +6,10 @@
 from jax.experimental.pallas import tpu as pltpu
 from jax.sharding import PartitionSpec as P
 
+
 PHI = 8192
 K = 33
-M = 2560
 LB = 64
-S_DEV = 4096
 RT = 128
 PER_DEV = 20
 ROWS = 32
@@ -75,22 +72,159 @@
     return lax.dot_general(x, y, (((1,), (1,)), ((), ())), preferred_element_type=jnp.float32)
 
 
-def spectra_kernel(
-    g_ref, kern_ref, mine_ref, fm_ref, fl_ref, w_ref, th_ref, tl_ref, out_ref,
-    s_ref, acc_ref, lt_ref, rt_ref, s1_ref, last_ref, zh_ref, zl_ref,
+def sort_kernel(
+    tod_h, cyc_h, phi_h, psi_h, off_h, cnt_ref, out_ref,
+    tod_ref, int_ref, data_ref, to_ref, o_ref, first_ref, first_s, buf_ref, sems,
 ):
-    mine = mine_ref[0]
+    copies = [pltpu.make_async_copy(tod_h, tod_ref, sems.at[0])]
+    for i, src in enumerate((cyc_h, phi_h, psi_h, off_h)):
+        copies.append(pltpu.make_async_copy(src, int_ref.at[i], sems.at[1 + i]))
+    for c in copies:
+        c.start()
+    for c in copies:
+        c.wait()
     slot = lax.broadcasted_iota(jnp.int32, (ROWS, 128), 0) * 128 + lax.broadcasted_iota(
         jnp.int32, (ROWS, 128), 1
     )
+    cyc = jnp.where(slot < cnt_ref[0, 0], int_ref[0], 4)
+
+    def below(n):
+        return (
+            lax.broadcasted_iota(jnp.int32, (n, n), 0) < lax.broadcasted_iota(jnp.int32, (n, n), 1)
+        ).astype(jnp.float32).astype(BF)
+
+    earlier = below(128)
+    rows_before = (
+        lax.broadcasted_iota(jnp.int32, (ROWS, ROWS), 1) < lax.broadcasted_iota(jnp.int32, (ROWS, ROWS), 0)
+    ).astype(jnp.float32).astype(BF)
+    every = jnp.ones((128, 128), BF)
+    lane0 = lax.broadcasted_iota(jnp.int32, (ROWS, 128), 1)
+    place = jnp.full((ROWS, 128), -1.0, jnp.float32)
+    for c in range(4):
+        mine = (cyc == c).astype(jnp.float32)
+        m = mine.astype(BF)
+        total = dot(m, every)
+        start = dot(rows_before, total.astype(BF))
+        first_ref[c * 40 : c * 40 + 32, :] = start.astype(jnp.int32)
+        first_ref[c * 40 + 32 : c * 40 + 40, :] = jnp.broadcast_to(
+            (start + total)[31:32].astype(jnp.int32), (8, 128)
+        )
+        pos = (start + dot(m, earlier)).astype(jnp.int32) & 127
+        place = jnp.where(cyc == c, (pos + c * 128).astype(jnp.float32), place)
+    to_smem = pltpu.make_async_copy(first_ref, first_s, sems.at[5])
+    to_smem.start()
+    place = place.astype(jnp.int32)
+    to_ref[0] = (place >> 4).astype(jnp.float32)
+    to_ref[1] = (place & 15).astype(jnp.float32)
+
+    def channel(i, x):
+        data_ref[pl.ds(i, ROWS, stride=8), :] = x
+
+    tod = tod_ref[...]
+    hi = tod.astype(BF).astype(jnp.float32)
+    mid = (tod - hi).astype(BF).astype(jnp.float32)
+    channel(0, hi)
+    channel(1, mid)
+    channel(2, tod - hi - mid)
+    channel(3, (int_ref[1] >> 7).astype(jnp.float32))
+    channel(4, (int_ref[1] & 127).astype(jnp.float32))
+    channel(5, int_ref[2].astype(jnp.float32))
+    channel(6, int_ref[3].astype(jnp.float32))
+    channel(7, jnp.zeros((ROWS, 128), jnp.float32))
+
+    sub = lax.broadcasted_iota(jnp.int32, (16, 128), 0).astype(jnp.float32).astype(BF)
+    zero = jnp.zeros((16, 128), BF)
+    one = jnp.ones((16, 128), BF)
+
+    def route(i, carry):
+        hi = jnp.broadcast_to(to_ref[0, pl.ds(i, 1), :], (16, 128)).astype(BF)
+        lo = jnp.broadcast_to(to_ref[1, pl.ds(i, 1), :], (16, 128)).astype(BF)
+        ones = jnp.where(lo == sub, one, zero)
+        chosen = jnp.concatenate([jnp.where(hi == float(h), ones, zero) for h in range(32)], 0)
+        row = data_ref[pl.ds(pl.multiple_of(i * 8, 8), 8), :].astype(BF)
+        o_ref[pl.ds(pl.multiple_of(i * 8, 8), 8), :] = dot_nt(row, chosen)
+        return carry
+
+    lax.fori_loop(0, ROWS, route, 0, unroll=4)
+    to_smem.wait()
+    lane = lax.broadcasted_iota(jnp.int32, (8, 128), 1)
+
+    def append(i, held):
+        out = []
+        for c in range(4):
+            begin = first_s[c * 40 + i, 0]
+            row = begin >> 7
+            moved = o_ref[pl.ds(pl.multiple_of(i * 8, 8), 8), c * 128 : (c + 1) * 128]
+            same = lane >= (begin & 127)
+            full = held[c] + jnp.where(same, moved, 0.0)
+            over = jnp.where(same, 0.0, moved)
+            at = pl.multiple_of((c * 34 + row) * 8, 8)
+            buf_ref[pl.ds(at, 8), :] = full
+            buf_ref[pl.ds(at + 8, 8), :] = over
+            crossed = (first_s[c * 40 + i + 1, 0] >> 7) > row
+            out.append(jnp.where(crossed, over, full))
+        return tuple(out)
+
+    lax.fori_loop(0, ROWS, append, (jnp.zeros((8, 128), jnp.float32),) * 4, unroll=4)
+    for c in range(4):
+        valid = slot < first_s[c * 40 + 32, 0]
+
+        def take(ch):
+            return buf_ref[pl.ds(c * 34 * 8 + ch, ROWS, stride=8), :]
+
+        out_ref[c, 0] = jnp.where(valid, take(0) + take(1) + take(2), 0.0)
+        out_ref[c, 1] = jnp.where(valid, take(3) * 128.0 + take(4), 0.0)
+        out_ref[c, 2] = jnp.where(valid, take(5), -1.0)
+        out_ref[c, 3] = jnp.where(valid, take(6), 0.0)
+
+
+def tables_kernel(
+    fm_h, fl_h, th_h, tl_h, kern_h, s1_ref, fl_ref, th_ref, tl_ref, kb_ref, fm_ref, kern_ref, sems
+):
+    pairs = (
+        (fm_h, fm_ref), (fl_h, fl_ref), (th_h, th_ref), (tl_h, tl_ref), (kern_h, kern_ref)
+    )
+    copies = [pltpu.make_async_copy(a, b, sems.at[i]) for i, (a, b) in enumerate(pairs)]
+    for c in copies:
+        c.start()
+    copies[0].wait()
+    lane = lax.broadcasted_iota(jnp.int32, (16, 1024), 1) & 31
+    lane = lane.astype(jnp.float32).astype(BF)
+    for q in range(32):
+        keep = lane == float(q)
+        for part in range(2):
+            s1_ref[part, q * 16 : (q + 1) * 16, :] = jnp.where(
+                keep, fm_ref[part], jnp.zeros((16, 1024), BF)
+            )
+    for c in copies[1:]:
+        c.wait()
+    for t in range(4):
+        for o in range(8):
+            kb_ref[t * 8 + o] = jnp.full((8, 128), kern_ref[t, o], jnp.float32)
+
+
+def spectra_kernel(
+    g_ref, s1_ref, fl_ref, th_ref, tl_ref, kb_ref, w_h, out_ref,
+    s_ref, acc_ref, lt_ref, rt_ref, last_ref, zh_ref, zl_ref, w_ref, w_sem,
+):
+    w_copy = pltpu.make_async_copy(w_h, w_ref, w_sem.at[0])
+    w_copy.start()
+    ends, skips = [], []
+    total = jnp.int32(0)
+    s_ref[0, 4 * ROWS : 4 * ROWS + 8, :] = jnp.full((8, 128), -1.0, jnp.float32)
+    for ch in range(1, 8):
+        s_ref[ch, 4 * ROWS : 4 * ROWS + 8, :] = jnp.zeros((8, 128), jnp.float32)
     for s in range(4):
         tod = g_ref[s, 0]
         phi = g_ref[s, 1].astype(jnp.int32)
         psi = g_ref[s, 2].astype(jnp.int32)
         off = g_ref[s, 3].astype(jnp.int32)
-        cyc = g_ref[s, 4].astype(jnp.int32)
-        cnt = g_ref[s, 5].astype(jnp.int32)
-        live = (slot < cnt) & (cyc == mine)
+        live = psi >= 0
+        count = jnp.sum(live.astype(jnp.float32)).astype(jnp.int32)
+        rows = (count + 127) >> 7
+        total = total + rows
+        ends.append(total)
+        skips.append(ROWS - rows)
         first = jnp.where(phi == 0, PHI - 1, phi - 1)
         b_hi = (first & 511) >> 4
         is_last = psi == 32
@@ -102,7 +236,8 @@
         for t in range(4):
             weight = jnp.zeros((ROWS, 128), jnp.float32)
             for o in range(8):
-                weight = jnp.where(off == o, kern_ref[o, t], weight)
+                entry = jnp.concatenate([kb_ref[t * 8 + o]] * (ROWS // 8), 0)
+                weight = jnp.where(off == o, entry, weight)
             s_ref[4 + t, at, :] = (tod * weight).astype(BF).astype(jnp.float32)
 
     acc_ref[...] = jnp.zeros_like(acc_ref)
@@ -110,11 +245,16 @@
     zero = jnp.zeros((16, 128), BF)
     one = jnp.ones((16, 128), BF)
 
-    def build(row0):
+    def build(first):
         for j in range(BLOCK):
+            f = first + j
+            r = f
+            for s in range(4):
+                r = r + jnp.where(f >= ends[s], skips[s], 0)
+            r = jnp.minimum(r, 4 * ROWS)
 
             def row(ch):
-                v = s_ref[ch, pl.ds(row0 + j, 1), :]
+                v = s_ref[ch, pl.ds(r, 1), :]
                 return jnp.broadcast_to(v, (16, 128)).astype(BF)
 
             n_hi, n_lo, m_hi, m_lo = row(0), row(1), row(2), row(3)
@@ -137,23 +277,12 @@
                 rt_ref[h * 16 : (h + 1) * 16, at] = jnp.where(here, main, rest)
                 before = here
 
-    def step(i, base):
-        build(base + i * BLOCK)
+    def step(i, carry):
+        build(i * BLOCK)
         acc_ref[...] += dot_nt(rt_ref[...], lt_ref[...])
-        return base
-
-    for s in range(4):
-        count = jnp.max(g_ref[s, 5, 0:8, :]).astype(jnp.int32)
-        lax.fori_loop(0, (count + BLOCK * 128 - 1) // (BLOCK * 128), step, s * ROWS)
-
-    lane = lax.broadcasted_iota(jnp.int32, (16, 1024), 1) & 31
-    lane = lane.astype(jnp.float32).astype(BF)
-    for q in range(32):
-        keep = lane == float(q)
-        for part in range(2):
-            s1_ref[part, q * 16 : (q + 1) * 16, :] = jnp.where(
-                keep, fm_ref[part], jnp.zeros((16, 1024), BF)
-            )
+        return carry
+
+    lax.fori_loop(0, (total + BLOCK - 1) // BLOCK, step, 0)
 
     def chunk(r0, at):
         tile = acc_ref[r0 : r0 + 16, (at // 8) * 128 : (at // 8) * 128 + 128]
@@ -200,6 +329,8 @@
                 zh_ref[at, g * 256 + 128 : g * 256 + 256] = ih[:, take]
                 zl_ref[at, g * 256 : g * 256 + 128] = rl[:, take]
                 zl_ref[at, g * 256 + 128 : g * 256 + 256] = il[:, take]
+
+    w_copy.wait()
 
     def put(s_to, tile_no, value):
         out_ref[pl.ds(s_to * TILES + tile_no, 32, stride=4 * TILES), :] = value
@@ -232,15 +363,26 @@
             put(s_to, 10, row)
 
 
-def sky_kernel(r_ref, wig_ref, beam_ref, d_ref, out_ref, wbuf, gh_ref, gl_ref, h_ref, bb_ref, sems):
+def early_kernel(beam_h, d_h, bb_ref, d_ref, beam_ref, sems):
+    copies = (
+        pltpu.make_async_copy(beam_h, beam_ref, sems.at[0]),
+        pltpu.make_async_copy(d_h, d_ref, sems.at[1]),
+    )
+    for c in copies:
+        c.start()
+    for c in copies:
+        c.wait()
+    beam = beam_ref[...].T
+    for k in range(K):
+        bb_ref[k] = jnp.broadcast_to(beam[:, k : k + 1], (LB, 128))
+
+
+def sky_kernel(r_ref, wig_h, bb_ref, d_ref, out_ref, wbuf, gh_ref, gl_ref, h_ref, sems):
     def fetch(m):
-        return pltpu.make_async_copy(wig_ref.at[m], wbuf.at[m], sems.at[m])
+        return pltpu.make_async_copy(wig_h.at[m], wbuf.at[m], sems.at[m])
 
     for m in range(PER_DEV):
         fetch(m).start()
-
-    for k in range(K):
-        bb_ref[k] = jnp.broadcast_to(beam_ref[:, k : k + 1], (LB, 128))
 
     def tile(t):
         return r_ref[pl.ds(t, 128, stride=TILES), :].T
@@ -293,63 +435,116 @@
     return pl.BlockSpec(memory_space=pltpu.VMEM)
 
 
-def spectra(gathered, kernel, mine):
+def hbm():
+    return pl.BlockSpec(memory_space=pltpu.HBM)
+
+
+def stay(*arrays):
+    return [pltpu.with_memory_space_constraint(jnp.asarray(x), pltpu.HBM) for x in arrays]
+
+
+def sort(tod, cycle, phi_cell, psi_bin, offset, counts):
+    return pl.pallas_call(
+        sort_kernel,
+        out_shape=jax.ShapeDtypeStruct((4, 4, ROWS, 128), jnp.float32),
+        in_specs=[hbm()] * 5 + [pl.BlockSpec(memory_space=pltpu.SMEM)],
+        out_specs=vmem(),
+        scratch_shapes=[
+            pltpu.VMEM((ROWS, 128), jnp.float32),
+            pltpu.VMEM((4, ROWS, 128), jnp.int32),
+            pltpu.VMEM((ROWS * 8, 128), jnp.float32),
+            pltpu.VMEM((2, ROWS, 128), jnp.float32),
+            pltpu.VMEM((ROWS * 8, 512), jnp.float32),
+            pltpu.VMEM((160, 128), jnp.int32),
+            pltpu.SMEM((160, 128), jnp.int32),
+            pltpu.VMEM((4 * 34 * 8, 128), jnp.float32),
+            pltpu.SemaphoreType.DMA((6,)),
+        ],
+        compiler_params=pltpu.CompilerParams(vmem_limit_bytes=8 << 20),
+        name="sort",
+    )(*stay(tod, cycle, phi_cell, psi_bin, offset), counts)
+
+
+def tables(kernel):
+    shapes = ((2, 512, 1024), F_LAST.shape, TW_HI.shape, TW_LO.shape, (32, 8, 128))
+    types = (BF, BF) + (jnp.float32,) * 3
+    return pl.pallas_call(
+        tables_kernel,
+        out_shape=[pltpu.VMEM(s, t) for s, t in zip(shapes, types)],
+        in_specs=[hbm()] * 5,
+        out_specs=[vmem()] * 5,
+        scratch_shapes=[
+            pltpu.VMEM((2, 16, 1024), BF),
+            pltpu.SMEM((4, 8), jnp.float32),
+            pltpu.SemaphoreType.DMA((5,)),
+        ],
+        compiler_params=pltpu.CompilerParams(vmem_limit_bytes=8 << 20),
+        name="tables",
+    )(*stay(F_MAIN, F_LAST, TW_HI, TW_LO, kernel))
+
+
+def spectra(gathered, *consts):
     return pl.pallas_call(
         spectra_kernel,
         out_shape=jax.ShapeDtypeStruct((128 * TILES, 128), jnp.float32),
-        in_specs=[
-            vmem(),
-            pl.BlockSpec(memory_space=pltpu.SMEM),
-            pl.BlockSpec(memory_space=pltpu.SMEM),
-            vmem(), vmem(), vmem(), vmem(), vmem(),
-        ],
+        in_specs=[vmem()] * 6 + [hbm()],
         out_specs=vmem(),
         scratch_shapes=[
-            pltpu.VMEM((8, 128, 128), jnp.float32),
+            pltpu.VMEM((8, 4 * ROWS + 8, 128), jnp.float32),
             pltpu.VMEM((CELL_ROWS, 512), jnp.float32),
             pltpu.VMEM((512, BLOCK * 128), BF),
             pltpu.VMEM((CELL_ROWS, BLOCK * 128), BF),
-            pltpu.VMEM((2, 512, 1024), BF),
             pltpu.VMEM((528, 128), jnp.float32),
             pltpu.VMEM((512, 1280), BF),
             pltpu.VMEM((512, 1280), BF),
+            pltpu.VMEM(W_PHI.shape, BF),
+            pltpu.SemaphoreType.DMA((1,)),
         ],
-        compiler_params=pltpu.CompilerParams(vmem_limit_bytes=32 << 20),
+        compiler_params=pltpu.CompilerParams(vmem_limit_bytes=20 << 20),
         name="spectra",
-    )(gathered, kernel, mine, F_MAIN, F_LAST, W_PHI, TW_HI, TW_LO)
-
-
-def sky_of(received, wigner, beam):
+    )(gathered, *consts, *stay(W_PHI))
+
+
+def early(beam):
+    return pl.pallas_call(
+        early_kernel,
+        out_shape=[pltpu.VMEM((K, LB, 128), jnp.float32), pltpu.VMEM(D_PSI.shape, BF)],
+        in_specs=[hbm()] * 2,
+        out_specs=[vmem()] * 2,
+        scratch_shapes=[pltpu.VMEM((K, LB), jnp.float32), pltpu.SemaphoreType.DMA((2,))],
+        compiler_params=pltpu.CompilerParams(vmem_limit_bytes=4 << 20),
+        name="early",
+    )(*stay(beam, D_PSI))
+
+
+def sky_of(received, wigner, bb, d):
     return pl.pallas_call(
         sky_kernel,
         out_shape=jax.ShapeDtypeStruct((PER_DEV, 2 * LB), jnp.float32),
-        in_specs=[vmem(), pl.BlockSpec(memory_space=pl.ANY), vmem(), vmem()],
+        in_specs=[vmem(), hbm(), vmem(), vmem()],
         out_specs=vmem(),
         scratch_shapes=[
             pltpu.VMEM((PER_DEV, K, LB, RT), jnp.float32),
             pltpu.VMEM((PER_DEV // 2, 80, 256), BF),
             pltpu.VMEM((PER_DEV // 2, 80, 256), BF),
             pltpu.VMEM((PER_DEV, 80, 128), jnp.float32),
-            pltpu.VMEM((K, LB, 128), jnp.float32),
             pltpu.SemaphoreType.DMA((PER_DEV,)),
         ],
-        compiler_params=pltpu.CompilerParams(vmem_limit_bytes=40 << 20),
+        compiler_params=pltpu.CompilerParams(vmem_limit_bytes=36 << 20),
         name="sky",
-    )(received, wigner, beam, D_PSI)
+    )(received, wigner, bb, d)
 
 
 def body(tod, cycle, phi_cell, psi_bin, offset, counts, kernel, wigner, beam):
-    rows = [
-        x.reshape(ROWS, 128).astype(jnp.float32) for x in (tod, phi_cell, psi_bin, offset, cycle)
-    ]
-    rows.append(jnp.broadcast_to(counts.astype(jnp.float32), (ROWS, 128)))
-    gathered = lax.all_gather(jnp.stack(rows), "samp")
-    mine = lax.axis_index("samp").astype(jnp.int32).reshape(1)
-    sent = spectra(gathered, kernel, mine)
-    received = lax.all_to_all(
-        sent.reshape(128, 1, TILES * 128), ("band", "samp"), 0, 0, tiled=True
-    ).reshape(128 * TILES, 128)
-    return sky_of(received, wigner[0], beam).reshape(1, PER_DEV, 2 * LB)
+    flat = [x.reshape(ROWS, 128) for x in (tod, cycle, phi_cell, psi_bin, offset)]
+    lists = sort(*flat, counts)
+    gathered = lax.all_to_all(lists, "samp", 0, 0, tiled=True)
+    consts = tables(kernel.T)
+    sent = spectra(gathered, *consts)
+    received = lax.all_to_all(sent.reshape(128, 1, TILES * 128), ("band", "samp"), 0, 0, tiled=True)
+    bb, d = early(beam.T)
+    sky = sky_of(received.reshape(128 * TILES, 128), wigner[0], bb, d)
+    return sky.reshape(1, PER_DEV, 2 * LB)
 
 
 def solution(mesh):

time: 77.7 us -> 59.8 us (0.77); the launches traced: 78.4 us -> 59.4 us
  blocking collectives: 12.1 us -> 0 us
  local copies, waits for them, and re-layouts: 8.34 us -> 0.61 us
  waiting for transfers between devices: 15 us -> 18.9 us
  other arithmetic: 2.93 us -> 0 us
    all_gather x1 -> x0, blocking collectives: 12.1 us -> none  [body(): gathered = lax.all_gather(jnp.stack(rows), 'samp')]
    unnamed x19 -> x0, local copies, waits for them, and re-layouts: 7.72 us -> none
    pallas_call x1, Pallas kernels: 15.9 us -> 8.25 us  [spectra(): pl.pallas_call(spectra_kernel, out_shape=jax.ShapeDtypeStruct((128 * TILE...]
    pallas_call x0 -> x3, Pallas kernels: none -> 6.99 us  [the longest x1 4.53 us: sort(): pl.pallas_call(sort_kernel, out_shape=jax.ShapeDtypeStruct((4, 4, ROWS, 1...]
    all_to_all x0 -> x1, starting transfers between devices: none -> 5.01 us  [body(): gathered = lax.all_to_all(lists, 'samp', 0, 0, tiled=True)]
    all_to_all x1, starting transfers between devices: 14.1 us -> 9.23 us  [body(): lax.all_to_all(sent.reshape(128, 1, TILES * 128), ('band', 'samp'), 0, 0,...]
    all_to_all x0 -> x1, waiting for transfers between devices: none -> 4.4 us  [body(): gathered = lax.all_to_all(lists, 'samp', 0, 0, tiled=True)]
    convert_element_type x4 -> x0, other arithmetic: 2.93 us -> none  [body(): x.reshape(ROWS, 128).astype(jnp.float32)]
  transfers between devices with their start and end apart: 1 -> 2, of which waited for: 1 -> 2; matrix products, arithmetic and copies ran while one was open for 1% -> 0% of each run, Pallas kernels for 0% -> 4%
where the time goes in v1:
time: 59.8 us; the launch traced here: 59.4 us
  Pallas kernels  24.9 us (42%)
  waiting for transfers between devices  18.9 us (32%)
  starting transfers between devices  14.2 us (24%)
  between operations  0.7 us (1%)
  local copies, waits for them, and re-layouts  0.61 us (1%)
    all_to_all x1, waiting for transfers between devices, body(): lax.all_to_all(sent.reshape(128, 1, TILES * 128), ('band', 'samp'), 0, 0,...  14.5 us
    pallas_call x1, Pallas kernels, sky_of(): pl.pallas_call(sky_kernel, out_shape=jax.ShapeDtypeStruct((PER_DEV, 2 * L...  9.68 us
    all_to_all x1, starting transfers between devices, body(): lax.all_to_all(sent.reshape(128, 1, TILES * 128), ('band', 'samp'), 0, 0,...  9.23 us
    pallas_call x1, Pallas kernels, spectra(): pl.pallas_call(spectra_kernel, out_shape=jax.ShapeDtypeStruct((128 * TILE...  8.25 us
    all_to_all x1, starting transfers between devices, body(): gathered = lax.all_to_all(lists, 'samp', 0, 0, tiled=True)  5.01 us
    pallas_call x1, Pallas kernels, sort(): pl.pallas_call(sort_kernel, out_shape=jax.ShapeDtypeStruct((4, 4, ROWS, 1...  4.53 us
    all_to_all x1, waiting for transfers between devices, body(): gathered = lax.all_to_all(lists, 'samp', 0, 0, tiled=True)  4.4 us
    pallas_call x1, Pallas kernels, early(): pl.pallas_call(early_kernel, out_shape=[pltpu.VMEM((K, LB, 128), jnp.floa...  1.31 us
  transfers between devices with their start and end apart: 2, of which 2 were waited for; matrix products, arithmetic and copies ran while one was open for 0% of the time, Pallas kernels for 4%

profile of v1, /device:TPU:1, one launch (start us, length us, event | category | flops | bytes accessed | tf_op | source)
XLA Modules:
  0.0 59.4 jit_solution(10572558778453062671)
XLA Ops:
  0.7 4.5 %sort.1 = f32[4,4,32,128]{3,2,1,0:T(8,128)} custom-call(f32[32,128]{1,0:T(8,128)} %bitcast.15, s32[32,128]{1,0:T(8,128)} %bitcast.16, s32[32,128]{1,0:T(8,128)} %bitcast.17, s32[32,128]{1,0:T(8,128)} %bitcast.18, s32[32,128]{1,0:T(8,128)} %bitcast.19, s32[1,1]{1,0:T(1,128)S(6)} %copy.19.cnt_ref), custom_call_target="tpu_custom_call" | custom-call | tf_op jit(solution)/shard_map/sort/pallas_call | solution.py:447
  5.2 5.0 %all-to-all-start = ((f32[4,4,32,128]{3,2,1,0:T(8,128)}), f32[4,4,32,128]{3,2,1,0:T(8,128)S(1)}, u32[]{:S(2)}, u32[]{:S(2)}) async-start(f32[4,4,32,128]{3,2,1,0:T(8,128)} %sort.1), calls=%async_computation | async-start | bytes 524288 | tf_op jit(solution)/shard_map/all_to_all | solution.py:541
  10.2 1.1 %tables.1 = (bf16[2,512,1024]{2,1,0:T(8,128)(2,1)S(1)}, bf16[2,128,256]{2,1,0:T(8,128)(2,1)S(1)}, f32[2,33,640]{2,1,0:T(8,128)S(1)}, f32[2,16,640]{2,1,0:T(8,128)S(1)}, f32[32,8,128]{2,1,0:T(8,128)S(1)}) custom-call(bf16[2,16,1024]{2,1,0:T(8,128)(2,1)} %constant.12.clone.fm_h, bf16[2,128,256]{2,1,0:T(8,128)(2,1)} %constant.13.clone.fl_h, ...), custom_call_target="tpu_custom_call" | custom-call | tf_op jit(solution)/shard_map/tables/pallas_call | solution.py:471
  11.4 4.4 %all-to-all-done.g_ref = f32[4,4,32,128]{3,2,1,0:T(8,128)S(1)} async-done(((f32[4,4,32,128]{3,2,1,0:T(8,128)}), f32[4,4,32,128]{3,2,1,0:T(8,128)S(1)}, u32[]{:S(2)}, u32[]{:S(2)}) %all-to-all-start) | async-done | bytes 262176 | tf_op jit(solution)/shard_map/all_to_all | solution.py:541
  15.8 8.3 %spectra.1 = f32[1408,128]{1,0:T(8,128)} custom-call(f32[4,4,32,128]{3,2,1,0:T(8,128)S(1)} %all-to-all-done.g_ref, bf16[2,512,1024]{2,1,0:T(8,128)(2,1)S(1)} %get-tuple-element.12.s1_ref, bf16[2,128,256]{2,1,0:T(8,128)(2,1)S(1)} %get-tuple-element.13.fl_ref, f32[2,33,640]{2,1,0:T(8,128)S(1)} %get-tuple-element.14.th_ref, ...), custom_call_target="tpu_custom_call" | custom-call | tf_op jit(solution)/shard_map/spectra/pallas_call | solution.py:487
  24.0 9.2 %all-to-all-start.1 = ((f32[128,1,1408]{2,1,0:T(1,128)}), f32[128,1,1408]{2,1,0:T(1,128)S(1)}, u32[]{:S(2)}, u32[]{:S(2)}) async-start(f32[128,1,1408]{2,1,0:T(1,128)} %bitcast.6), calls=%async_computation.1 | async-start | bytes 1441792 | tf_op jit(solution)/shard_map/all_to_all | solution.py:544
  33.3 1.3 %early.1 = (f32[33,64,128]{2,1,0:T(8,128)S(1)}, bf16[2,80,80]{2,1,0:T(8,128)(2,1)S(1)}) custom-call(f32[33,64]{1,0:T(8,128)} %bitcast.14, bf16[2,80,80]{2,1,0:T(8,128)(2,1)} %constant.17.clone.d_h), custom_call_target="tpu_custom_call" | custom-call | tf_op jit(solution)/shard_map/early/pallas_call | solution.py:509
  34.6 14.5 %all-to-all-done.1 = f32[128,1,1408]{2,1,0:T(1,128)S(1)} async-done(((f32[128,1,1408]{2,1,0:T(1,128)}), f32[128,1,1408]{2,1,0:T(1,128)S(1)}, u32[]{:S(2)}, u32[]{:S(2)}) %all-to-all-start.1) | async-done | bytes 720928 | tf_op jit(solution)/shard_map/all_to_all | solution.py:544
  49.1 9.7 %sky.1 = f32[20,128]{1,0:T(8,128)S(1)} custom-call(f32[1408,128]{1,0:T(8,128)S(1)} %bitcast.11, f32[20,33,64,128]{3,2,1,0:T(8,128)} %bitcast.13, f32[33,64,128]{2,1,0:T(8,128)S(1)} %get-tuple-element.17.bb_ref, bf16[2,80,80]{2,1,0:T(8,128)(2,1)S(1)} %get-tuple-element.18.d_ref), custom_call_target="tpu_custom_call" | custom-call | tf_op jit(solution)/shard_map/sky/pallas_call | solution.py:521
  58.8 0.6 %copy.18 = f32[1,20,128]{2,0,1:T(1,128)} copy(f32[1,20,128]{2,1,0:T(8,128)S(1)} %bitcast.12) | data formatting | bytes 20480 | tf_op jit(solution)/shard_map/reshape | solution.py:547
Async XLA Ops:
  5.2 10.6 %all-to-all-start = ((f32[4,4,32,128]{3,2,1,0:T(8,128)}), f32[4,4,32,128]{3,2,1,0:T(8,128)S(1)}, u32[]{:S(2)}, u32[]{:S(2)}) async-start(f32[4,4,32,128]{3,2,1,0:T(8,128)} %sort.1), calls=%async_computation | async-start | bytes 524288 | tf_op jit(solution)/shard_map/all_to_all | solution.py:541
  24.0 25.1 %all-to-all-start.1 = ((f32[128,1,1408]{2,1,0:T(1,128)}), f32[128,1,1408]{2,1,0:T(1,128)S(1)}, u32[]{:S(2)}, u32[]{:S(2)}) async-start(f32[128,1,1408]{2,1,0:T(1,128)} %bitcast.6), calls=%async_computation.1 | async-start | bytes 1441792 | tf_op jit(solution)/shard_map/all_to_all | solution.py:544

commit v2 on v1

--- a/solution.py
+++ b/solution.py
@@ -16,6 +16,9 @@
 BLOCK = 4
 CELL_ROWS = 560
 TILES = 11
+HEAD = 2
+WROWS = K * LB
+WPAD = WROWS + 8
 BF = jnp.bfloat16
 
 
@@ -31,7 +34,8 @@
     cl = np.arange(16)
     ang = 2 * np.pi * ((a[:, None] * cl[None, :]) % 16) / 16
     fc, fs = np.cos(ang), -np.sin(ang)
-    f_main = np.concatenate([np.repeat(fc, 32, 1), np.repeat(fs, 32, 1)], 1)
+    packed = np.concatenate([fc[:, :8], fc[:, 8:9], fs[:, 1:8]], 1)
+    f_main = np.repeat(packed, 32, 1)
     f_last = np.zeros((128, 256))
     f_last[:16, :16] = fc
     f_last[:16, 128:144] = fs
@@ -73,7 +77,7 @@
 
 
 def sort_kernel(
-    tod_h, cyc_h, phi_h, psi_h, off_h, cnt_ref, out_ref,
+    tod_h, cyc_h, phi_h, psi_h, off_h, cnt_ref, mine_ref, out0, out1, out2, out3,
     tod_ref, int_ref, data_ref, to_ref, o_ref, first_ref, first_s, buf_ref, sems,
 ):
     copies = [pltpu.make_async_copy(tod_h, tod_ref, sems.at[0])]
@@ -86,7 +90,7 @@
     slot = lax.broadcasted_iota(jnp.int32, (ROWS, 128), 0) * 128 + lax.broadcasted_iota(
         jnp.int32, (ROWS, 128), 1
     )
-    cyc = jnp.where(slot < cnt_ref[0, 0], int_ref[0], 4)
+    cyc = jnp.where(slot < cnt_ref[0, 0], (int_ref[0] - mine_ref[0]) & 3, 4)
 
     def below(n):
         return (
@@ -166,16 +170,16 @@
         return tuple(out)
 
     lax.fori_loop(0, ROWS, append, (jnp.zeros((8, 128), jnp.float32),) * 4, unroll=4)
-    for c in range(4):
+    for c, out_ref in enumerate((out0, out1, out2, out3)):
         valid = slot < first_s[c * 40 + 32, 0]
 
         def take(ch):
             return buf_ref[pl.ds(c * 34 * 8 + ch, ROWS, stride=8), :]
 
-        out_ref[c, 0] = jnp.where(valid, take(0) + take(1) + take(2), 0.0)
-        out_ref[c, 1] = jnp.where(valid, take(3) * 128.0 + take(4), 0.0)
-        out_ref[c, 2] = jnp.where(valid, take(5), -1.0)
-        out_ref[c, 3] = jnp.where(valid, take(6), 0.0)
+        out_ref[0] = jnp.where(valid, take(0) + take(1) + take(2), 0.0)
+        out_ref[1] = jnp.where(valid, take(3) * 128.0 + take(4), 0.0)
+        out_ref[2] = jnp.where(valid, take(5), -1.0)
+        out_ref[3] = jnp.where(valid, take(6), 0.0)
 
 
 def tables_kernel(
@@ -188,13 +192,13 @@
     for c in copies:
         c.start()
     copies[0].wait()
-    lane = lax.broadcasted_iota(jnp.int32, (16, 1024), 1) & 31
+    lane = lax.broadcasted_iota(jnp.int32, (16, 512), 1) & 31
     lane = lane.astype(jnp.float32).astype(BF)
     for q in range(32):
         keep = lane == float(q)
         for part in range(2):
             s1_ref[part, q * 16 : (q + 1) * 16, :] = jnp.where(
-                keep, fm_ref[part], jnp.zeros((16, 1024), BF)
+                keep, fm_ref[part], jnp.zeros((16, 512), BF)
             )
     for c in copies[1:]:
         c.wait()
@@ -204,7 +208,7 @@
 
 
 def spectra_kernel(
-    g_ref, s1_ref, fl_ref, th_ref, tl_ref, kb_ref, w_h, out_ref,
+    g0, g1, g2, g3, s1_ref, fl_ref, th_ref, tl_ref, kb_ref, w_h, out_ref,
     s_ref, acc_ref, lt_ref, rt_ref, last_ref, zh_ref, zl_ref, w_ref, w_sem,
 ):
     w_copy = pltpu.make_async_copy(w_h, w_ref, w_sem.at[0])
@@ -214,11 +218,11 @@
     s_ref[0, 4 * ROWS : 4 * ROWS + 8, :] = jnp.full((8, 128), -1.0, jnp.float32)
     for ch in range(1, 8):
         s_ref[ch, 4 * ROWS : 4 * ROWS + 8, :] = jnp.zeros((8, 128), jnp.float32)
-    for s in range(4):
-        tod = g_ref[s, 0]
-        phi = g_ref[s, 1].astype(jnp.int32)
-        psi = g_ref[s, 2].astype(jnp.int32)
-        off = g_ref[s, 3].astype(jnp.int32)
+    for s, g_ref in enumerate((g0, g1, g2, g3)):
+        tod = g_ref[0]
+        phi = g_ref[1].astype(jnp.int32)
+        psi = g_ref[2].astype(jnp.int32)
+        off = g_ref[3].astype(jnp.int32)
         live = psi >= 0
         count = jnp.sum(live.astype(jnp.float32)).astype(jnp.int32)
         rows = (count + 127) >> 7
@@ -297,6 +301,12 @@
             tile = tile + chunk(544, h - 1)
         last_ref[h * 16 : (h + 1) * 16, :] = tile
 
+    quarter = lax.broadcasted_iota(jnp.int32, (16, 128), 1) >> 5
+    none = jnp.zeros((16, 128), jnp.float32)
+
+    def pick(at0, at2, odd):
+        return jnp.where(quarter == 0, at0, jnp.where(quarter == 2, at2, odd))
+
     def first_stage(r0, rows):
         at = pl.ds(r0, rows)
         xh, xl = split(acc_ref[at, :])
@@ -310,8 +320,14 @@
             cw = ch * tl_ref[0] - sh * tl_ref[1]
             sw = sh * tl_ref[0] + ch * tl_ref[1]
             at = slice(i * 16, (i + 1) * 16)
-            yr = jnp.concatenate([y[at, :512], y_last[at, :128]], 1)
-            yi = jnp.concatenate([y[at, 512:], y_last[at, 128:]], 1)
+            a0, a1, b0, b1 = (y[at, g * 128 : (g + 1) * 128] for g in range(4))
+            ra0, ra1, rb0, rb1 = (pltpu.roll(v, 64, 1) for v in (a0, a1, b0, b1))
+            yr = jnp.concatenate(
+                [a0, a1, pick(b0, a1, ra1), pick(a1, a0, ra0), y_last[at, :128]], 1
+            )
+            yi = jnp.concatenate(
+                [pick(none, b0, b0), b1, -pick(none, b1, rb1), -pick(b1, b0, rb0), y_last[at, 128:]], 1
+            )
             out.append((yr * cw + yi * sw, yi * cw - yr * sw))
         return out
 
@@ -363,26 +379,32 @@
             put(s_to, 10, row)
 
 
-def early_kernel(beam_h, d_h, bb_ref, d_ref, beam_ref, sems):
-    copies = (
-        pltpu.make_async_copy(beam_h, beam_ref, sems.at[0]),
-        pltpu.make_async_copy(d_h, d_ref, sems.at[1]),
-    )
+def early_kernel(wig_h, d_h, head_ref, d_ref, sems):
+    copies = [pltpu.make_async_copy(d_h, d_ref, sems.at[HEAD])]
+    for m in range(HEAD):
+        copies.append(
+            pltpu.make_async_copy(wig_h.at[m], head_ref.at[m, pl.ds(0, WROWS)], sems.at[m])
+        )
     for c in copies:
         c.start()
     for c in copies:
         c.wait()
+
+
+def sky_kernel(
+    r_ref, wig_h, head_ref, beam_ref, d_ref, out_h, wbuf, bb_ref, gh_ref, gl_ref, h_ref, out_ref, sems, out_sem
+):
+    def fetch(m):
+        return pltpu.make_async_copy(
+            wig_h.at[m], wbuf.at[m - HEAD, pl.ds(0, WROWS)], sems.at[m - HEAD]
+        )
+
+    for m in range(HEAD, PER_DEV):
+        fetch(m).start()
+
     beam = beam_ref[...].T
     for k in range(K):
-        bb_ref[k] = jnp.broadcast_to(beam[:, k : k + 1], (LB, 128))
-
-
-def sky_kernel(r_ref, wig_h, bb_ref, d_ref, out_ref, wbuf, gh_ref, gl_ref, h_ref, sems):
-    def fetch(m):
-        return pltpu.make_async_copy(wig_h.at[m], wbuf.at[m], sems.at[m])
-
-    for m in range(PER_DEV):
-        fetch(m).start()
+        bb_ref[k * LB : (k + 1) * LB, :] = jnp.broadcast_to(beam[:, k : k + 1], (LB, 128))
 
     def tile(t):
         return r_ref[pl.ds(t, 128, stride=TILES), :].T
@@ -409,26 +431,44 @@
 
     ones = jnp.ones((16, 128), BF)
 
-    def order(m, carry):
+    def orders(m, w_ref, at_m):
+        sums = [[jnp.zeros((8, 128), jnp.float32)] * 16 for _ in range(2)]
+        for k in range(K):
+            h = [
+                [
+                    jnp.broadcast_to(h_ref[m + n, 2 * k + c : 2 * k + c + 1, :], (8, 128))
+                    for c in range(2)
+                ]
+                for n in range(2)
+            ]
+            for i in range(8):
+                row = k * LB + i * 8
+                b = bb_ref[row : row + 8, :]
+                for n in range(2):
+                    w = w_ref[at_m + n, row : row + 8, :] * b
+                    sums[n][i] = sums[n][i] + w * h[n][0]
+                    sums[n][8 + i] = sums[n][8 + i] + w * h[n][1]
+        for n in range(2):
+            both = jnp.concatenate(sums[n], 0)
+            hi, lo = split(both)
+            tail = (both - hi.astype(jnp.float32) - lo.astype(jnp.float32)).astype(BF)
+            res = dot_nt(ones, hi) + dot_nt(ones, lo) + dot_nt(ones, tail)
+            out_ref[m + n] = res[0:1]
+
+    for m in range(0, HEAD, 2):
+        orders(m, head_ref, m)
+
+    def streamed(i, carry):
+        m = HEAD + 2 * i
         fetch(m).wait()
-        real = [jnp.zeros((8, 128), jnp.float32)] * 8
-        imag = [jnp.zeros((8, 128), jnp.float32)] * 8
-        for k in range(K):
-            hr = jnp.broadcast_to(h_ref[m, 2 * k : 2 * k + 1, :], (8, 128))
-            hi = jnp.broadcast_to(h_ref[m, 2 * k + 1 : 2 * k + 2, :], (8, 128))
-            for i in range(8):
-                at = slice(i * 8, (i + 1) * 8)
-                w = wbuf[m, k, at, :] * bb_ref[k, at, :]
-                real[i] = real[i] + w * hr
-                imag[i] = imag[i] + w * hi
-        both = jnp.concatenate(real + imag, 0)
-        hi, lo = split(both)
-        tail = (both - hi.astype(jnp.float32) - lo.astype(jnp.float32)).astype(BF)
-        res = dot_nt(ones, hi) + dot_nt(ones, lo) + dot_nt(ones, tail)
-        out_ref[pl.ds(m, 1), :] = res[0:1]
+        fetch(m + 1).wait()
+        orders(m, wbuf, 2 * i)
         return carry
 
-    lax.fori_loop(0, PER_DEV, order, 0)
+    lax.fori_loop(0, (PER_DEV - HEAD) // 2, streamed, 0)
+    out_copy = pltpu.make_async_copy(out_ref, out_h, out_sem.at[0])
+    out_copy.start()
+    out_copy.wait()
 
 
 def vmem():
@@ -443,12 +483,12 @@
     return [pltpu.with_memory_space_constraint(jnp.asarray(x), pltpu.HBM) for x in arrays]
 
 
-def sort(tod, cycle, phi_cell, psi_bin, offset, counts):
+def sort(tod, cycle, phi_cell, psi_bin, offset, counts, mine):
     return pl.pallas_call(
         sort_kernel,
-        out_shape=jax.ShapeDtypeStruct((4, 4, ROWS, 128), jnp.float32),
-        in_specs=[hbm()] * 5 + [pl.BlockSpec(memory_space=pltpu.SMEM)],
-        out_specs=vmem(),
+        out_shape=[jax.ShapeDtypeStruct((4, ROWS, 128), jnp.float32)] * 4,
+        in_specs=[hbm()] * 5 + [pl.BlockSpec(memory_space=pltpu.SMEM)] * 2,
+        out_specs=[vmem()] * 4,
         scratch_shapes=[
             pltpu.VMEM((ROWS, 128), jnp.float32),
             pltpu.VMEM((4, ROWS, 128), jnp.int32),
@@ -462,11 +502,11 @@
         ],
         compiler_params=pltpu.CompilerParams(vmem_limit_bytes=8 << 20),
         name="sort",
-    )(*stay(tod, cycle, phi_cell, psi_bin, offset), counts)
+    )(*stay(tod, cycle, phi_cell, psi_bin, offset), counts, mine)
 
 
 def tables(kernel):
-    shapes = ((2, 512, 1024), F_LAST.shape, TW_HI.shape, TW_LO.shape, (32, 8, 128))
+    shapes = ((2, 512, 512), F_LAST.shape, TW_HI.shape, TW_LO.shape, (32, 8, 128))
     types = (BF, BF) + (jnp.float32,) * 3
     return pl.pallas_call(
         tables_kernel,
@@ -474,7 +514,7 @@
         in_specs=[hbm()] * 5,
         out_specs=[vmem()] * 5,
         scratch_shapes=[
-            pltpu.VMEM((2, 16, 1024), BF),
+            pltpu.VMEM((2, 16, 512), BF),
             pltpu.SMEM((4, 8), jnp.float32),
             pltpu.SemaphoreType.DMA((5,)),
         ],
@@ -483,11 +523,11 @@
     )(*stay(F_MAIN, F_LAST, TW_HI, TW_LO, kernel))
 
 
-def spectra(gathered, *consts):
+def spectra(lists, *consts):
     return pl.pallas_call(
         spectra_kernel,
         out_shape=jax.ShapeDtypeStruct((128 * TILES, 128), jnp.float32),
-        in_specs=[vmem()] * 6 + [hbm()],
+        in_specs=[vmem()] * 9 + [hbm()],
         out_specs=vmem(),
         scratch_shapes=[
             pltpu.VMEM((8, 4 * ROWS + 8, 128), jnp.float32),
@@ -502,49 +542,56 @@
         ],
         compiler_params=pltpu.CompilerParams(vmem_limit_bytes=20 << 20),
         name="spectra",
-    )(gathered, *consts, *stay(W_PHI))
-
-
-def early(beam):
+    )(*lists, *consts, *stay(W_PHI))
+
+
+def early(wigner):
     return pl.pallas_call(
         early_kernel,
-        out_shape=[pltpu.VMEM((K, LB, 128), jnp.float32), pltpu.VMEM(D_PSI.shape, BF)],
+        out_shape=[pltpu.VMEM((HEAD, WPAD, RT), jnp.float32), pltpu.VMEM(D_PSI.shape, BF)],
         in_specs=[hbm()] * 2,
         out_specs=[vmem()] * 2,
-        scratch_shapes=[pltpu.VMEM((K, LB), jnp.float32), pltpu.SemaphoreType.DMA((2,))],
+        scratch_shapes=[pltpu.SemaphoreType.DMA((HEAD + 1,))],
         compiler_params=pltpu.CompilerParams(vmem_limit_bytes=4 << 20),
         name="early",
-    )(*stay(beam, D_PSI))
-
-
-def sky_of(received, wigner, bb, d):
+    )(*stay(wigner, D_PSI))
+
+
+def sky_of(received, wigner, head, beam, d):
     return pl.pallas_call(
         sky_kernel,
-        out_shape=jax.ShapeDtypeStruct((PER_DEV, 2 * LB), jnp.float32),
-        in_specs=[vmem(), hbm(), vmem(), vmem()],
-        out_specs=vmem(),
+        out_shape=pltpu.HBM((PER_DEV, 1, 2 * LB), jnp.float32),
+        in_specs=[vmem(), hbm(), vmem(), vmem(), vmem()],
+        out_specs=hbm(),
         scratch_shapes=[
-            pltpu.VMEM((PER_DEV, K, LB, RT), jnp.float32),
+            pltpu.VMEM((PER_DEV - HEAD, WPAD, RT), jnp.float32),
+            pltpu.VMEM((WROWS, 128), jnp.float32),
             pltpu.VMEM((PER_DEV // 2, 80, 256), BF),
             pltpu.VMEM((PER_DEV // 2, 80, 256), BF),
             pltpu.VMEM((PER_DEV, 80, 128), jnp.float32),
-            pltpu.SemaphoreType.DMA((PER_DEV,)),
+            pltpu.VMEM((PER_DEV, 1, 2 * LB), jnp.float32),
+            pltpu.SemaphoreType.DMA((PER_DEV - HEAD,)),
+            pltpu.SemaphoreType.DMA((1,)),
         ],
         compiler_params=pltpu.CompilerParams(vmem_limit_bytes=36 << 20),
         name="sky",
-    )(received, wigner, bb, d)
+    )(received, *stay(wigner), head, beam, d)
 
 
 def body(tod, cycle, phi_cell, psi_bin, offset, counts, kernel, wigner, beam):
     flat = [x.reshape(ROWS, 128) for x in (tod, cycle, phi_cell, psi_bin, offset)]
-    lists = sort(*flat, counts)
-    gathered = lax.all_to_all(lists, "samp", 0, 0, tiled=True)
+    mine = lax.axis_index("samp").astype(jnp.int32).reshape(1)
+    lists = sort(*flat, counts, mine)
+    gathered = [lists[0]] + [
+        lax.ppermute(lists[d], "samp", [(i, (i + d) % 4) for i in range(4)]) for d in (2, 1, 3)
+    ]
     consts = tables(kernel.T)
     sent = spectra(gathered, *consts)
     received = lax.all_to_all(sent.reshape(128, 1, TILES * 128), ("band", "samp"), 0, 0, tiled=True)
-    bb, d = early(beam.T)
-    sky = sky_of(received.reshape(128 * TILES, 128), wigner[0], bb, d)
-    return sky.reshape(1, PER_DEV, 2 * LB)
+    wigner = wigner.reshape(PER_DEV, WROWS, RT)
+    head, d = early(wigner)
+    sky = sky_of(received.reshape(128 * TILES, 128), wigner, head, beam.T, d)
+    return jnp.transpose(sky, (1, 0, 2))
 
 
 def solution(mesh):

time: 59.8 us -> 56.4 us (0.943)
  waiting for transfers between devices: 18.9 us -> 14.7 us
  starting transfers between devices: 14.2 us -> 17.8 us
  Pallas kernels: 24.9 us -> 22.8 us
  local copies, waits for them, and re-layouts: 0.61 us -> 0.01 us
    ppermute x0 -> x3, starting transfers between devices: none -> 6.49 us  [body(): lax.ppermute(lists[d], 'samp', [(i, (i + d) % 4) for i in range(4)])]
    all_to_all x1 -> x0, starting transfers between devices: 5.01 us -> none  [body(): gathered = lax.all_to_all(lists, 'samp', 0, 0, tiled=True)]
    all_to_all x1 -> x0, waiting for transfers between devices: 4.4 us -> none  [body(): gathered = lax.all_to_all(lists, 'samp', 0, 0, tiled=True)]
    all_to_all x1, starting transfers between devices: 9.23 us -> 11.3 us  [body(): lax.all_to_all(sent.reshape(128, 1, TILES * 128), ('band', 'samp'), 0, 0,...]
    pallas_call x1, Pallas kernels: 8.25 us -> 7.19 us  [spectra(): pl.pallas_call(spectra_kernel, out_shape=jax.ShapeDtypeStruct((128 * TILE...]
    pallas_call x3, Pallas kernels: 15.5 us -> 14.5 us  [the longest x1 9.04 us: sky_of(): pl.pallas_call(sky_kernel, out_shape=pltpu.HBM((PER_DEV, 1, 2 * LB), jnp....]
    reshape x1 -> x0, local copies, waits for them, and re-layouts: 0.61 us -> none  [body(): return sky.reshape(1, PER_DEV, 2 * LB)]
  transfers between devices with their start and end apart: 2 -> 4, of which waited for: 2 -> 2; matrix products, arithmetic and copies ran while one was open for 0% -> 0% of each run, Pallas kernels for 4% -> 5%
where the time goes in v2:
time: 56.4 us; the launch traced here: 56.1 us
  Pallas kernels  22.8 us (40%)
  starting transfers between devices  17.8 us (32%)
  waiting for transfers between devices  14.7 us (26%)
  between operations  0.71 us (1%)
    all_to_all x1, waiting for transfers between devices, body(): lax.all_to_all(sent.reshape(128, 1, TILES * 128), ('band', 'samp'), 0, 0,...  14.2 us
    all_to_all x1, starting transfers between devices, body(): lax.all_to_all(sent.reshape(128, 1, TILES * 128), ('band', 'samp'), 0, 0,...  11.3 us
    pallas_call x1, Pallas kernels, sky_of(): pl.pallas_call(sky_kernel, out_shape=pltpu.HBM((PER_DEV, 1, 2 * LB), jnp....  9.04 us
    pallas_call x1, Pallas kernels, spectra(): pl.pallas_call(spectra_kernel, out_shape=jax.ShapeDtypeStruct((128 * TILE...  7.19 us
    ppermute x3, starting transfers between devices, body(): lax.ppermute(lists[d], 'samp', [(i, (i + d) % 4) for i in range(4)])  6.49 us
    pallas_call x1, Pallas kernels, sort(): pl.pallas_call(sort_kernel, out_shape=[jax.ShapeDtypeStruct((4, ROWS, 128...  3.84 us
    pallas_call x1, Pallas kernels, early(): pl.pallas_call(early_kernel, out_shape=[pltpu.VMEM((HEAD, WPAD, RT), jnp....  1.62 us
    pallas_call x1, Pallas kernels, tables(): pl.pallas_call(tables_kernel, out_shape=[pltpu.VMEM(s, t) for s, t in zip...  1.13 us
  transfers between devices with their start and end apart: 4, of which 2 were waited for; matrix products, arithmetic and copies ran while one was open for 0% of the time, Pallas kernels for 5%

profile of v2, /device:TPU:1, one launch (start us, length us, event | category | flops | bytes accessed | tf_op | source)
XLA Modules:
  0.0 56.1 jit_solution(1527530491582641358)
XLA Ops:
  0.0 0.0 copy-start
  0.7 3.8 %sort.1 = (f32[4,32,128]{2,1,0:T(8,128)S(1)}, f32[4,32,128]{2,1,0:T(8,128)S(1)}, f32[4,32,128]{2,1,0:T(8,128)S(1)}, f32[4,32,128]{2,1,0:T(8,128)S(1)}) custom-call(f32[32,128]{1,0:T(8,128)} %bitcast.16, s32[32,128]{1,0:T(8,128)} %bitcast.17, s32[32,128]{1,0:T(8,128)} %bitcast.18, s32[32,128]{1,0:T(8,128)} %bitcast.19, s32[32,128]{1,0:T(8,128)} %bitcast.20, ...), custom_call_target="tpu_custom_call" | custom-call | tf_op jit(solution)/shard_map/sort/pallas_call | solution.py:487
  4.5 3.8 %collective-permute-start = (f32[4,32,128]{2,1,0:T(8,128)S(1)}, f32[4,32,128]{2,1,0:T(8,128)S(1)}, u32[]{:S(2)}, u32[]{:S(2)}) collective-permute-start(f32[4,32,128]{2,1,0:T(8,128)S(1)} %get-tuple-element.17), channel_id=1, source_target_pairs={{0,64},{32,96},{64,0},{96,32},{1,65},{33,97},{65,1},{97,33},{2,66}... | collective-permute-start | bytes 196616 | tf_op jit(solution)/shard_map/ppermute | solution.py:586
  8.3 0.4 collective-permute-start.1
  8.7 2.3 %collective-permute-start.2 = (f32[4,32,128]{2,1,0:T(8,128)S(1)}, f32[4,32,128]{2,1,0:T(8,128)S(1)}, u32[]{:S(2)}, u32[]{:S(2)}) collective-permute-start(f32[4,32,128]{2,1,0:T(8,128)S(1)} %get-tuple-element.19), channel_id=1, source_target_pairs={{0,96},{32,0},{64,32},{96,64},{1,97},{33,1},{65,33},{97,65},{2,98}... | collective-permute-start | bytes 196616 | tf_op jit(solution)/shard_map/ppermute | solution.py:586
  11.0 1.1 %tables.1 = (bf16[2,512,512]{2,1,0:T(8,128)(2,1)S(1)}, bf16[2,128,256]{2,1,0:T(8,128)(2,1)S(1)}, f32[2,33,640]{2,1,0:T(8,128)S(1)}, f32[2,16,640]{2,1,0:T(8,128)S(1)}, f32[32,8,128]{2,1,0:T(8,128)S(1)}) custom-call(bf16[2,16,512]{2,1,0:T(8,128)(2,1)} %constant.18.clone.fm_h, bf16[2,128,256]{2,1,0:T(8,128)(2,1)} %constant.19.clone.fl_h, ...), custom_call_target="tpu_custom_call" | custom-call | tf_op jit(solution)/shard_map/tables/pallas_call | solution.py:511
  12.1 0.0 collective-permute-done.g1
  12.1 0.5 collective-permute-done.1.g2
  12.6 0.0 collective-permute-done.2.g3
  12.7 7.2 %spectra.1 = f32[1408,128]{1,0:T(8,128)} custom-call(f32[4,32,128]{2,1,0:T(8,128)S(1)} %get-tuple-element.16.g0, f32[4,32,128]{2,1,0:T(8,128)S(1)} %collective-permute-done.g1, f32[4,32,128]{2,1,0:T(8,128)S(1)} %collective-permute-done.1.g2, f32[4,32,128]{2,1,0:T(8,128)S(1)} %collective-permute-done.2.g3, bf16[2,512,512]{2,1,0:T(8,128)(2,1)S(1)} %get-tuple-element.20.s1_ref, ...), custom_call_target="tpu_custom_call" | custom-call | tf_op jit(solution)/shard_map/spectra/pallas_call | solution.py:527
  19.9 11.3 %all-to-all-start = ((f32[128,1,1408]{2,1,0:T(1,128)}), f32[128,1,1408]{2,1,0:T(1,128)S(1)}, u32[]{:S(2)}, u32[]{:S(2)}) async-start(f32[128,1,1408]{2,1,0:T(1,128)} %bitcast.7), calls=%async_computation | async-start | bytes 1441792 | tf_op jit(solution)/shard_map/all_to_all | solution.py:590
  31.2 1.6 %early.1 = (f32[2,2120,128]{2,1,0:T(8,128)S(1)}, bf16[2,80,80]{2,1,0:T(8,128)(2,1)S(1)}) custom-call(f32[20,2112,128]{2,1,0:T(8,128)} %bitcast.14, bf16[2,80,80]{2,1,0:T(8,128)(2,1)} %constant.23.clone.d_h), custom_call_target="tpu_custom_call" | custom-call | tf_op jit(solution)/shard_map/early/pallas_call | solution.py:549
  32.8 14.2 %all-to-all-done = f32[128,1,1408]{2,1,0:T(1,128)S(1)} async-done(((f32[128,1,1408]{2,1,0:T(1,128)}), f32[128,1,1408]{2,1,0:T(1,128)S(1)}, u32[]{:S(2)}, u32[]{:S(2)}) %all-to-all-start) | async-done | bytes 720928 | tf_op jit(solution)/shard_map/all_to_all | solution.py:590
  47.0 0.0 copy-done
  47.0 9.0 %sky.1 = f32[20,1,128]{2,1,0:T(1,128)} custom-call(f32[1408,128]{1,0:T(8,128)S(1)} %bitcast.12, f32[20,2112,128]{2,1,0:T(8,128)} %bitcast.15, f32[2,2120,128]{2,1,0:T(8,128)S(1)} %get-tuple-element.25.head_ref, f32[33,64]{1,0:T(8,128)S(1)} %bitcast.13, bf16[2,80,80]{2,1,0:T(8,128)(2,1)S(1)} %get-tuple-element.26.d_ref), custom_call_target="tpu_custom_call" | custom-call | tf_op jit(solution)/shard_map/sky/pallas_call | solution.py:561
Async XLA Ops:
  0.0 47.0 %copy-start = (f32[64,33]{0,1:T(8,128)S(1)}, f32[64,33]{0,1:T(8,128)}, u32[]{:S(2)}) copy-start(f32[64,33]{0,1:T(8,128)} %param.23) | copy-start | bytes 25348
  4.5 7.6 %collective-permute-start = (f32[4,32,128]{2,1,0:T(8,128)S(1)}, f32[4,32,128]{2,1,0:T(8,128)S(1)}, u32[]{:S(2)}, u32[]{:S(2)}) collective-permute-start(f32[4,32,128]{2,1,0:T(8,128)S(1)} %get-tuple-element.17), channel_id=1, source_target_pairs={{0,64},{32,96},{64,0},{96,32},{1,65},{33,97},{65,1},{97,33},{2,66}... | collective-permute-start | bytes 196616 | tf_op jit(solution)/shard_map/ppermute | solution.py:586
  8.3 4.3 %collective-permute-start.1 = (f32[4,32,128]{2,1,0:T(8,128)S(1)}, f32[4,32,128]{2,1,0:T(8,128)S(1)}, u32[]{:S(2)}, u32[]{:S(2)}) collective-permute-start(f32[4,32,128]{2,1,0:T(8,128)S(1)} %get-tuple-element.18), channel_id=1, source_target_pairs={{0,32},{32,64},{64,96},{96,0},{1,33},{33,65},{65,97},{97,1},{2,34}... | collective-permute-start | bytes 196616 | tf_op jit(solution)/shard_map/ppermute | solution.py:586
  8.7 3.9 %collective-permute-start.2 = (f32[4,32,128]{2,1,0:T(8,128)S(1)}, f32[4,32,128]{2,1,0:T(8,128)S(1)}, u32[]{:S(2)}, u32[]{:S(2)}) collective-permute-start(f32[4,32,128]{2,1,0:T(8,128)S(1)} %get-tuple-element.19), channel_id=1, source_target_pairs={{0,96},{32,0},{64,32},{96,64},{1,97},{33,1},{65,33},{97,65},{2,98}... | collective-permute-start | bytes 196616 | tf_op jit(solution)/shard_map/ppermute | solution.py:586
  19.9 27.2 %all-to-all-start = ((f32[128,1,1408]{2,1,0:T(1,128)}), f32[128,1,1408]{2,1,0:T(1,128)S(1)}, u32[]{:S(2)}, u32[]{:S(2)}) async-start(f32[128,1,1408]{2,1,0:T(1,128)} %bitcast.7), calls=%async_computation | async-start | bytes 1441792 | tf_op jit(solution)/shard_map/all_to_all | solution.py:590

commit v3 on v2

--- a/solution.py
+++ b/solution.py
@@ -13,10 +13,11 @@
 RT = 128
 PER_DEV = 20
 ROWS = 32
-BLOCK = 4
+BLOCK = 8
 CELL_ROWS = 560
 TILES = 11
 HEAD = 2
+KSTEP = 11
 WROWS = K * LB
 WPAD = WROWS + 8
 BF = jnp.bfloat16
@@ -209,7 +210,7 @@
 
 def spectra_kernel(
     g0, g1, g2, g3, s1_ref, fl_ref, th_ref, tl_ref, kb_ref, w_h, out_ref,
-    s_ref, acc_ref, lt_ref, rt_ref, last_ref, zh_ref, zl_ref, w_ref, w_sem,
+    s_ref, acc_ref, last_ref, zh_ref, zl_ref, w_ref, w_sem,
 ):
     w_copy = pltpu.make_async_copy(w_h, w_ref, w_sem.at[0])
     w_copy.start()
@@ -250,6 +251,7 @@
     one = jnp.ones((16, 128), BF)
 
     def build(first):
+        left, right = [], []
         for j in range(BLOCK):
             f = first + j
             r = f
@@ -271,19 +273,29 @@
             spill = jnp.where(
                 d == -15.0, a1, jnp.where(d == -14.0, a2, jnp.where(d == -13.0, a3, zero))
             )
-            at = pl.ds(j * 128, 128)
-            for h in range(32):
-                lt_ref[h * 16 : (h + 1) * 16, at] = jnp.where(n_hi == float(h), ones, zero)
-            before = None
-            for h in range(35):
-                here = m_hi == float(h)
-                rest = zero if before is None else jnp.where(before, spill, zero)
-                rt_ref[h * 16 : (h + 1) * 16, at] = jnp.where(here, main, rest)
-                before = here
+            left.append(jnp.concatenate([jnp.where(n_hi == float(h), ones, zero) for h in range(32)], 0))
+            here = [m_hi == float(h) for h in range(35)]
+            right.append(
+                jnp.concatenate(
+                    [jnp.where(here[0], main, zero)]
+                    + [
+                        jnp.where(here[h], main, jnp.where(here[h - 1], spill, zero))
+                        for h in range(1, 35)
+                    ],
+                    0,
+                )
+            )
+        return left, right
 
     def step(i, carry):
-        build(i * BLOCK)
-        acc_ref[...] += dot_nt(rt_ref[...], lt_ref[...])
+        left, right = build(i * BLOCK)
+        total = None
+        for j in range(0, BLOCK, 2):
+            part = dot_nt(
+                jnp.concatenate(right[j : j + 2], 1), jnp.concatenate(left[j : j + 2], 1)
+            )
+            total = part if total is None else total + part
+        acc_ref[...] += total
         return carry
 
     lax.fori_loop(0, (total + BLOCK - 1) // BLOCK, step, 0)
@@ -432,22 +444,28 @@
     ones = jnp.ones((16, 128), BF)
 
     def orders(m, w_ref, at_m):
-        sums = [[jnp.zeros((8, 128), jnp.float32)] * 16 for _ in range(2)]
-        for k in range(K):
-            h = [
-                [
-                    jnp.broadcast_to(h_ref[m + n, 2 * k + c : 2 * k + c + 1, :], (8, 128))
-                    for c in range(2)
+        def some(kk, sums):
+            sums = [list(x) for x in sums]
+            for j in range(KSTEP):
+                k = kk * KSTEP + j
+                base = pl.multiple_of(k * LB, LB)
+                h = [
+                    [
+                        jnp.broadcast_to(h_ref[m + n, pl.ds(2 * k + c, 1), :], (8, 128))
+                        for c in range(2)
+                    ]
+                    for n in range(2)
                 ]
-                for n in range(2)
-            ]
-            for i in range(8):
-                row = k * LB + i * 8
-                b = bb_ref[row : row + 8, :]
-                for n in range(2):
-                    w = w_ref[at_m + n, row : row + 8, :] * b
-                    sums[n][i] = sums[n][i] + w * h[n][0]
-                    sums[n][8 + i] = sums[n][8 + i] + w * h[n][1]
+                for i in range(8):
+                    b = bb_ref[pl.ds(base + i * 8, 8), :]
+                    for n in range(2):
+                        w = w_ref[at_m + n, pl.ds(base + i * 8, 8), :] * b
+                        sums[n][i] = sums[n][i] + w * h[n][0]
+                        sums[n][8 + i] = sums[n][8 + i] + w * h[n][1]
+            return tuple(tuple(x) for x in sums)
+
+        sums = ((jnp.zeros((8, 128), jnp.float32),) * 16,) * 2
+        sums = lax.fori_loop(0, K // KSTEP, some, sums)
         for n in range(2):
             both = jnp.concatenate(sums[n], 0)
             hi, lo = split(both)
@@ -532,8 +550,6 @@
         scratch_shapes=[
             pltpu.VMEM((8, 4 * ROWS + 8, 128), jnp.float32),
             pltpu.VMEM((CELL_ROWS, 512), jnp.float32),
-            pltpu.VMEM((512, BLOCK * 128), BF),
-            pltpu.VMEM((CELL_ROWS, BLOCK * 128), BF),
             pltpu.VMEM((528, 128), jnp.float32),
             pltpu.VMEM((512, 1280), BF),
             pltpu.VMEM((512, 1280), BF),

time: 56.4 us -> 55.2 us (0.979)
  Pallas kernels: 22.8 us -> 21.6 us
    pallas_call x1, Pallas kernels: 9.04 us -> 8.15 us  [sky_of(): pl.pallas_call(sky_kernel, out_shape=pltpu.HBM((PER_DEV, 1, 2 * LB), jnp....]
where the time goes in v3:
time: 55.2 us; the launch traced here: 54.9 us
  Pallas kernels  21.6 us (39%)
  starting transfers between devices  17.8 us (32%)
  waiting for transfers between devices  14.7 us (27%)
  between operations  0.71 us (1%)
    all_to_all x1, waiting for transfers between devices, body(): lax.all_to_all(sent.reshape(128, 1, TILES * 128), ('band', 'samp'), 0, 0,...  14.2 us
    all_to_all x1, starting transfers between devices, body(): lax.all_to_all(sent.reshape(128, 1, TILES * 128), ('band', 'samp'), 0, 0,...  11.3 us
    pallas_call x1, Pallas kernels, sky_of(): pl.pallas_call(sky_kernel, out_shape=pltpu.HBM((PER_DEV, 1, 2 * LB), jnp....  8.15 us
    pallas_call x1, Pallas kernels, spectra(): pl.pallas_call(spectra_kernel, out_shape=jax.ShapeDtypeStruct((128 * TILE...  6.89 us
    ppermute x3, starting transfers between devices, body(): lax.ppermute(lists[d], 'samp', [(i, (i + d) % 4) for i in range(4)])  6.49 us
    pallas_call x1, Pallas kernels, sort(): pl.pallas_call(sort_kernel, out_shape=[jax.ShapeDtypeStruct((4, ROWS, 128...  3.84 us
    pallas_call x1, Pallas kernels, early(): pl.pallas_call(early_kernel, out_shape=[pltpu.VMEM((HEAD, WPAD, RT), jnp....  1.62 us
    pallas_call x1, Pallas kernels, tables(): pl.pallas_call(tables_kernel, out_shape=[pltpu.VMEM(s, t) for s, t in zip...  1.13 us
  transfers between devices with their start and end apart: 4, of which 2 were waited for; matrix products, arithmetic and copies ran while one was open for 0% of the time, Pallas kernels for 5%

profile of v3, /device:TPU:1, one launch (start us, length us, event | category | flops | bytes accessed | tf_op | source)
XLA Modules:
  0.0 54.9 jit_solution(17897839815375425476)
XLA Ops:
  0.0 0.0 copy-start
  0.7 3.8 %sort.1 = (f32[4,32,128]{2,1,0:T(8,128)S(1)}, f32[4,32,128]{2,1,0:T(8,128)S(1)}, f32[4,32,128]{2,1,0:T(8,128)S(1)}, f32[4,32,128]{2,1,0:T(8,128)S(1)}) custom-call(f32[32,128]{1,0:T(8,128)} %bitcast.16, s32[32,128]{1,0:T(8,128)} %bitcast.17, s32[32,128]{1,0:T(8,128)} %bitcast.18, s32[32,128]{1,0:T(8,128)} %bitcast.19, s32[32,128]{1,0:T(8,128)} %bitcast.20, ...), custom_call_target="tpu_custom_call" | custom-call | tf_op jit(solution)/shard_map/sort/pallas_call | solution.py:505
  4.5 3.8 %collective-permute-start = (f32[4,32,128]{2,1,0:T(8,128)S(1)}, f32[4,32,128]{2,1,0:T(8,128)S(1)}, u32[]{:S(2)}, u32[]{:S(2)}) collective-permute-start(f32[4,32,128]{2,1,0:T(8,128)S(1)} %get-tuple-element.17), channel_id=1, source_target_pairs={{0,64},{32,96},{64,0},{96,32},{1,65},{33,97},{65,1},{97,33},{2,66}... | collective-permute-start | bytes 196616 | tf_op jit(solution)/shard_map/ppermute | solution.py:602
  8.3 0.4 collective-permute-start.1
  8.7 2.3 %collective-permute-start.2 = (f32[4,32,128]{2,1,0:T(8,128)S(1)}, f32[4,32,128]{2,1,0:T(8,128)S(1)}, u32[]{:S(2)}, u32[]{:S(2)}) collective-permute-start(f32[4,32,128]{2,1,0:T(8,128)S(1)} %get-tuple-element.19), channel_id=1, source_target_pairs={{0,96},{32,0},{64,32},{96,64},{1,97},{33,1},{65,33},{97,65},{2,98}... | collective-permute-start | bytes 196616 | tf_op jit(solution)/shard_map/ppermute | solution.py:602
  11.0 1.1 %tables.1 = (bf16[2,512,512]{2,1,0:T(8,128)(2,1)S(1)}, bf16[2,128,256]{2,1,0:T(8,128)(2,1)S(1)}, f32[2,33,640]{2,1,0:T(8,128)S(1)}, f32[2,16,640]{2,1,0:T(8,128)S(1)}, f32[32,8,128]{2,1,0:T(8,128)S(1)}) custom-call(bf16[2,16,512]{2,1,0:T(8,128)(2,1)} %constant.18.clone.fm_h, bf16[2,128,256]{2,1,0:T(8,128)(2,1)} %constant.19.clone.fl_h, ...), custom_call_target="tpu_custom_call" | custom-call | tf_op jit(solution)/shard_map/tables/pallas_call | solution.py:529
  12.1 0.0 collective-permute-done.g1
  12.1 0.5 collective-permute-done.1.g2
  12.6 0.0 collective-permute-done.2.g3
  12.7 6.9 %spectra.1 = f32[1408,128]{1,0:T(8,128)} custom-call(f32[4,32,128]{2,1,0:T(8,128)S(1)} %get-tuple-element.16.g0, f32[4,32,128]{2,1,0:T(8,128)S(1)} %collective-permute-done.g1, f32[4,32,128]{2,1,0:T(8,128)S(1)} %collective-permute-done.1.g2, f32[4,32,128]{2,1,0:T(8,128)S(1)} %collective-permute-done.2.g3, bf16[2,512,512]{2,1,0:T(8,128)(2,1)S(1)} %get-tuple-element.20.s1_ref, ...), custom_call_target="tpu_custom_call" | custom-call | tf_op jit(solution)/shard_map/spectra/pallas_call | solution.py:545
  19.5 11.3 %all-to-all-start = ((f32[128,1,1408]{2,1,0:T(1,128)}), f32[128,1,1408]{2,1,0:T(1,128)S(1)}, u32[]{:S(2)}, u32[]{:S(2)}) async-start(f32[128,1,1408]{2,1,0:T(1,128)} %bitcast.7), calls=%async_computation | async-start | bytes 1441792 | tf_op jit(solution)/shard_map/all_to_all | solution.py:606
  30.9 1.6 %early.1 = (f32[2,2120,128]{2,1,0:T(8,128)S(1)}, bf16[2,80,80]{2,1,0:T(8,128)(2,1)S(1)}) custom-call(f32[20,2112,128]{2,1,0:T(8,128)} %bitcast.14, bf16[2,80,80]{2,1,0:T(8,128)(2,1)} %constant.23.clone.d_h), custom_call_target="tpu_custom_call" | custom-call | tf_op jit(solution)/shard_map/early/pallas_call | solution.py:565
  32.5 14.2 %all-to-all-done = f32[128,1,1408]{2,1,0:T(1,128)S(1)} async-done(((f32[128,1,1408]{2,1,0:T(1,128)}), f32[128,1,1408]{2,1,0:T(1,128)S(1)}, u32[]{:S(2)}, u32[]{:S(2)}) %all-to-all-start) | async-done | bytes 720928 | tf_op jit(solution)/shard_map/all_to_all | solution.py:606
  46.7 0.0 copy-done
  46.7 8.1 %sky.1 = f32[20,1,128]{2,1,0:T(1,128)} custom-call(f32[1408,128]{1,0:T(8,128)S(1)} %bitcast.12, f32[20,2112,128]{2,1,0:T(8,128)} %bitcast.15, f32[2,2120,128]{2,1,0:T(8,128)S(1)} %get-tuple-element.25.head_ref, f32[33,64]{1,0:T(8,128)S(1)} %bitcast.13, bf16[2,80,80]{2,1,0:T(8,128)(2,1)S(1)} %get-tuple-element.26.d_ref), custom_call_target="tpu_custom_call" | custom-call | tf_op jit(solution)/shard_map/sky/pallas_call | solution.py:577
Async XLA Ops:
  0.0 46.7 %copy-start = (f32[64,33]{0,1:T(8,128)S(1)}, f32[64,33]{0,1:T(8,128)}, u32[]{:S(2)}) copy-start(f32[64,33]{0,1:T(8,128)} %param.23) | copy-start | bytes 25348
  4.5 7.6 %collective-permute-start = (f32[4,32,128]{2,1,0:T(8,128)S(1)}, f32[4,32,128]{2,1,0:T(8,128)S(1)}, u32[]{:S(2)}, u32[]{:S(2)}) collective-permute-start(f32[4,32,128]{2,1,0:T(8,128)S(1)} %get-tuple-element.17), channel_id=1, source_target_pairs={{0,64},{32,96},{64,0},{96,32},{1,65},{33,97},{65,1},{97,33},{2,66}... | collective-permute-start | bytes 196616 | tf_op jit(solution)/shard_map/ppermute | solution.py:602
  8.3 4.3 %collective-permute-start.1 = (f32[4,32,128]{2,1,0:T(8,128)S(1)}, f32[4,32,128]{2,1,0:T(8,128)S(1)}, u32[]{:S(2)}, u32[]{:S(2)}) collective-permute-start(f32[4,32,128]{2,1,0:T(8,128)S(1)} %get-tuple-element.18), channel_id=1, source_target_pairs={{0,32},{32,64},{64,96},{96,0},{1,33},{33,65},{65,97},{97,1},{2,34}... | collective-permute-start | bytes 196616 | tf_op jit(solution)/shard_map/ppermute | solution.py:602
  8.7 3.9 %collective-permute-start.2 = (f32[4,32,128]{2,1,0:T(8,128)S(1)}, f32[4,32,128]{2,1,0:T(8,128)S(1)}, u32[]{:S(2)}, u32[]{:S(2)}) collective-permute-start(f32[4,32,128]{2,1,0:T(8,128)S(1)} %get-tuple-element.19), channel_id=1, source_target_pairs={{0,96},{32,0},{64,32},{96,64},{1,97},{33,1},{65,33},{97,65},{2,98}... | collective-permute-start | bytes 196616 | tf_op jit(solution)/shard_map/ppermute | solution.py:602
  19.5 27.2 %all-to-all-start = ((f32[128,1,1408]{2,1,0:T(1,128)}), f32[128,1,1408]{2,1,0:T(1,128)S(1)}, u32[]{:S(2)}, u32[]{:S(2)}) async-start(f32[128,1,1408]{2,1,0:T(1,128)} %bitcast.7), calls=%async_computation | async-start | bytes 1441792 | tf_op jit(solution)/shard_map/all_to_all | solution.py:606

commit v4 on v3

--- a/solution.py
+++ b/solution.py
@@ -40,10 +40,14 @@
     f_last = np.zeros((128, 256))
     f_last[:16, :16] = fc
     f_last[:16, 128:144] = fs
-    b = np.arange(512)
-    m2 = (5 * np.arange(32)[None, :] + np.arange(5)[:, None]).reshape(-1)
-    ang = 2 * np.pi * ((m2[:, None] * b[None, :]) % 512) / 512
-    w_phi = np.concatenate([np.cos(ang), np.sin(ang)], 0)
+    b = np.arange(256)
+    e, i = np.arange(5)[:, None], np.arange(16)[None, :]
+    halves = []
+    for odd in range(2):
+        m2 = (5 * (2 * i + (e + odd) % 2) + e).reshape(-1)
+        ang = 2 * np.pi * ((m2[:, None] * b[None, :]) % 512) / 512
+        halves.append(np.concatenate([np.cos(ang), np.sin(ang)], 0))
+    w_phi = np.stack(halves)
     lanes = np.concatenate([np.arange(512) // 32, np.where(np.arange(128) < 16, np.arange(128), 0)])
     ang = 2 * np.pi * (16 * np.arange(33)[:, None] * lanes[None, :]) / PHI
     t_hi = np.stack([np.cos(ang), np.sin(ang)]).astype(np.float32)
@@ -104,18 +108,23 @@
     ).astype(jnp.float32).astype(BF)
     every = jnp.ones((128, 128), BF)
     lane0 = lax.broadcasted_iota(jnp.int32, (ROWS, 128), 1)
+    row0 = lax.broadcasted_iota(jnp.int32, (ROWS, 128), 0)
     place = jnp.full((ROWS, 128), -1.0, jnp.float32)
+    ahead = jnp.zeros((ROWS, 128), jnp.float32)
+    starts, shifts = [], []
+
+    def on_lanes(x, shift):
+        return jnp.sum(jnp.where(lane0 == row0 + shift, x, 0.0), axis=0, keepdims=True)
+
     for c in range(4):
-        mine = (cyc == c).astype(jnp.float32)
-        m = mine.astype(BF)
+        m = (cyc == c).astype(jnp.float32).astype(BF)
         total = dot(m, every)
         start = dot(rows_before, total.astype(BF))
-        first_ref[c * 40 : c * 40 + 32, :] = start.astype(jnp.int32)
-        first_ref[c * 40 + 32 : c * 40 + 40, :] = jnp.broadcast_to(
-            (start + total)[31:32].astype(jnp.int32), (8, 128)
-        )
-        pos = (start + dot(m, earlier)).astype(jnp.int32) & 127
-        place = jnp.where(cyc == c, (pos + c * 128).astype(jnp.float32), place)
+        starts.append(on_lanes(start + total, 1))
+        shifts.append(on_lanes(start - ahead, 0))
+        place = jnp.where(cyc == c, ahead + dot(m, earlier), place)
+        ahead = ahead + total
+    first_ref[...] = jnp.concatenate(starts + shifts, 0).astype(jnp.int32)
     to_smem = pltpu.make_async_copy(first_ref, first_s, sems.at[5])
     to_smem.start()
     place = place.astype(jnp.int32)
@@ -145,34 +154,36 @@
         hi = jnp.broadcast_to(to_ref[0, pl.ds(i, 1), :], (16, 128)).astype(BF)
         lo = jnp.broadcast_to(to_ref[1, pl.ds(i, 1), :], (16, 128)).astype(BF)
         ones = jnp.where(lo == sub, one, zero)
-        chosen = jnp.concatenate([jnp.where(hi == float(h), ones, zero) for h in range(32)], 0)
+        chosen = jnp.concatenate([jnp.where(hi == float(h), ones, zero) for h in range(8)], 0)
         row = data_ref[pl.ds(pl.multiple_of(i * 8, 8), 8), :].astype(BF)
         o_ref[pl.ds(pl.multiple_of(i * 8, 8), 8), :] = dot_nt(row, chosen)
         return carry
 
-    lax.fori_loop(0, ROWS, route, 0, unroll=4)
+    lax.fori_loop(0, ROWS, route, 0, unroll=ROWS)
     to_smem.wait()
     lane = lax.broadcasted_iota(jnp.int32, (8, 128), 1)
 
     def append(i, held):
         out = []
+        moved = o_ref[pl.ds(pl.multiple_of(i * 8, 8), 8), :]
         for c in range(4):
-            begin = first_s[c * 40 + i, 0]
+            begin = first_s[c, i]
+            after = first_s[c, i + 1]
             row = begin >> 7
-            moved = o_ref[pl.ds(pl.multiple_of(i * 8, 8), 8), c * 128 : (c + 1) * 128]
-            same = lane >= (begin & 127)
-            full = held[c] + jnp.where(same, moved, 0.0)
-            over = jnp.where(same, 0.0, moved)
+            here = begin & 127
+            end = here + after - begin
+            own = pltpu.roll(moved, first_s[4 + c, i] & 127, 1)
+            full = held[c] + jnp.where((lane >= here) & (lane < end), own, 0.0)
+            over = jnp.where(lane < end - 128, own, 0.0)
             at = pl.multiple_of((c * 34 + row) * 8, 8)
             buf_ref[pl.ds(at, 8), :] = full
             buf_ref[pl.ds(at + 8, 8), :] = over
-            crossed = (first_s[c * 40 + i + 1, 0] >> 7) > row
-            out.append(jnp.where(crossed, over, full))
+            out.append(jnp.where((after >> 7) > row, over, full))
         return tuple(out)
 
-    lax.fori_loop(0, ROWS, append, (jnp.zeros((8, 128), jnp.float32),) * 4, unroll=4)
+    lax.fori_loop(0, ROWS, append, (jnp.zeros((8, 128), jnp.float32),) * 4, unroll=ROWS)
     for c, out_ref in enumerate((out0, out1, out2, out3)):
-        valid = slot < first_s[c * 40 + 32, 0]
+        valid = slot < first_s[c, ROWS]
 
         def take(ch):
             return buf_ref[pl.ds(c * 34 * 8 + ch, ROWS, stride=8), :]
@@ -344,51 +355,61 @@
         return out
 
     halo = first_stage(512, 16)[0]
-    for r0 in range(0, 512, 128):
-        for i, (zr, zi) in enumerate(first_stage(r0, 128)):
+    for r0 in range(0, 256, 128):
+        for i, (near, far) in enumerate(zip(first_stage(r0, 128), first_stage(r0 + 256, 128))):
             if r0 == 0 and i == 0:
-                zr, zi = zr + halo[0], zi + halo[1]
-            rh, rl = split(zr)
-            ih, il = split(zi)
+                near = (near[0] + halo[0], near[1] + halo[1])
             at = slice(r0 + i * 16, r0 + (i + 1) * 16)
-            for g in range(5):
-                take = slice(g * 128, (g + 1) * 128)
-                zh_ref[at, g * 256 : g * 256 + 128] = rh[:, take]
-                zh_ref[at, g * 256 + 128 : g * 256 + 256] = ih[:, take]
-                zl_ref[at, g * 256 : g * 256 + 128] = rl[:, take]
-                zl_ref[at, g * 256 + 128 : g * 256 + 256] = il[:, take]
+            for odd in range(2):
+                zr, zi = (n - f if odd else n + f for n, f in zip(near, far))
+                rh, rl = split(zr)
+                ih, il = split(zi)
+                for g in range(5):
+                    take = slice(g * 128, (g + 1) * 128)
+                    re, im = slice(g * 256, g * 256 + 128), slice(g * 256 + 128, g * 256 + 256)
+                    zh_ref[odd, at, re] = rh[:, take]
+                    zh_ref[odd, at, im] = ih[:, take]
+                    zl_ref[odd, at, re] = rl[:, take]
+                    zl_ref[odd, at, im] = il[:, take]
 
     w_copy.wait()
 
-    def put(s_to, tile_no, value):
-        out_ref[pl.ds(s_to * TILES + tile_no, 32, stride=4 * TILES), :] = value
-
+    def put(s_to, tile_no, half, value):
+        first = (4 * half + s_to) * TILES + tile_no
+        out_ref[pl.ds(first, 16, stride=8 * TILES), :] = value
+
+    lanes = lax.broadcasted_iota(jnp.int32, (16, 128), 1)
+    last_parts = [[[None] * 5 for _ in range(2)] for _ in range(2)]
     for g in range(5):
         take = slice(g * 256, (g + 1) * 256)
-        zh, zl = zh_ref[:, take], zl_ref[:, take]
-        p = dot(w_ref[0], zh) + dot(w_ref[1], zh) + dot(w_ref[0], zl)
-        parts = (p[:160, :128] + p[160:, 128:], p[:160, 128:] - p[160:, :128])
-        if g < 4:
+        for odd in range(2):
+            zh, zl = zh_ref[odd, :, take], zl_ref[odd, :, take]
+            p = dot(w_ref[0, odd], zh) + dot(w_ref[1, odd], zh) + dot(w_ref[0, odd], zl)
+            parts = (p[:80, :128] + p[80:, 128:], p[:80, 128:] - p[80:, :128])
+            if g < 4:
+                for c in range(2):
+                    for e in range(5):
+                        s_to, t = divmod(e * 4 + g, 5)
+                        put(s_to, c * 5 + t, (e + odd) % 2, parts[c][e * 16 : (e + 1) * 16])
+                continue
             for c in range(2):
                 for e in range(5):
-                    s_to, t = divmod(e * 4 + g, 5)
-                    put(s_to, c * 5 + t, parts[c][e * 32 : (e + 1) * 32])
-            continue
-        lanes = lax.broadcasted_iota(jnp.int32, (32, 128), 1)
-        for s_to in range(4):
-            row = jnp.zeros((32, 128), jnp.float32)
+                    last_parts[odd][c][e] = parts[c][e * 16 : (e + 1) * 16]
+    for s_to in range(4):
+        for half in range(2):
+            row = jnp.zeros((16, 128), jnp.float32)
             for c in range(2):
                 j = 0
                 while j < PER_DEV:
                     e, cl = divmod(PER_DEV * s_to + j, 16)
                     length = min(16 - cl, PER_DEV - j)
                     to = 64 * c + j
-                    piece = parts[c][e * 32 : (e + 1) * 32]
+                    piece = last_parts[(e + half) % 2][c][e]
                     shift = (to - cl) % 128
                     piece = piece if shift == 0 else pltpu.roll(piece, shift, 1)
                     row = jnp.where((lanes >= to) & (lanes < to + length), piece, row)
                     j += length
-            put(s_to, 10, row)
+            put(s_to, 10, half, row)
 
 
 def early_kernel(wig_h, d_h, head_ref, d_ref, sems):
@@ -512,9 +533,9 @@
             pltpu.VMEM((4, ROWS, 128), jnp.int32),
             pltpu.VMEM((ROWS * 8, 128), jnp.float32),
             pltpu.VMEM((2, ROWS, 128), jnp.float32),
-            pltpu.VMEM((ROWS * 8, 512), jnp.float32),
-            pltpu.VMEM((160, 128), jnp.int32),
-            pltpu.SMEM((160, 128), jnp.int32),
+            pltpu.VMEM((ROWS * 8, 128), jnp.float32),
+            pltpu.VMEM((8, 128), jnp.int32),
+            pltpu.SMEM((8, 128), jnp.int32),
             pltpu.VMEM((4 * 34 * 8, 128), jnp.float32),
             pltpu.SemaphoreType.DMA((6,)),
         ],
@@ -551,8 +572,8 @@
             pltpu.VMEM((8, 4 * ROWS + 8, 128), jnp.float32),
             pltpu.VMEM((CELL_ROWS, 512), jnp.float32),
             pltpu.VMEM((528, 128), jnp.float32),
-            pltpu.VMEM((512, 1280), BF),
-            pltpu.VMEM((512, 1280), BF),
+            pltpu.VMEM((2, 256, 1280), BF),
+            pltpu.VMEM((2, 256, 1280), BF),
             pltpu.VMEM(W_PHI.shape, BF),
             pltpu.SemaphoreType.DMA((1,)),
         ],

time: 55.2 us -> 53.4 us (0.967)
  Pallas kernels: 21.6 us -> 19.8 us
    pallas_call x1, Pallas kernels: 3.84 us -> 2.4 us  [sort(): pl.pallas_call(sort_kernel, out_shape=[jax.ShapeDtypeStruct((4, ROWS, 128...]
where the time goes in v4:
time: 53.4 us; the launch traced here: 53.1 us
  Pallas kernels  19.8 us (37%)
  starting transfers between devices  17.8 us (33%)
  waiting for transfers between devices  14.7 us (28%)
  between operations  0.71 us (1%)
    all_to_all x1, waiting for transfers between devices, body(): lax.all_to_all(sent.reshape(128, 1, TILES * 128), ('band', 'samp'), 0, 0,...  14.2 us
    all_to_all x1, starting transfers between devices, body(): lax.all_to_all(sent.reshape(128, 1, TILES * 128), ('band', 'samp'), 0, 0,...  11.3 us
    pallas_call x1, Pallas kernels, sky_of(): pl.pallas_call(sky_kernel, out_shape=pltpu.HBM((PER_DEV, 1, 2 * LB), jnp....  8.15 us
    pallas_call x1, Pallas kernels, spectra(): pl.pallas_call(spectra_kernel, out_shape=jax.ShapeDtypeStruct((128 * TILE...  6.51 us
    ppermute x3, starting transfers between devices, body(): lax.ppermute(lists[d], 'samp', [(i, (i + d) % 4) for i in range(4)])  6.49 us
    pallas_call x1, Pallas kernels, sort(): pl.pallas_call(sort_kernel, out_shape=[jax.ShapeDtypeStruct((4, ROWS, 128...  2.4 us
    pallas_call x1, Pallas kernels, early(): pl.pallas_call(early_kernel, out_shape=[pltpu.VMEM((HEAD, WPAD, RT), jnp....  1.62 us
    pallas_call x1, Pallas kernels, tables(): pl.pallas_call(tables_kernel, out_shape=[pltpu.VMEM(s, t) for s, t in zip...  1.13 us
  transfers between devices with their start and end apart: 4, of which 2 were waited for; matrix products, arithmetic and copies ran while one was open for 0% of the time, Pallas kernels for 5%

profile of v4, /device:TPU:1, one launch (start us, length us, event | category | flops | bytes accessed | tf_op | source)
XLA Modules:
  0.0 53.1 jit_solution(3471767975669150878)
XLA Ops:
  0.0 0.0 copy-start
  0.7 2.4 %sort.1 = (f32[4,32,128]{2,1,0:T(8,128)S(1)}, f32[4,32,128]{2,1,0:T(8,128)S(1)}, f32[4,32,128]{2,1,0:T(8,128)S(1)}, f32[4,32,128]{2,1,0:T(8,128)S(1)}) custom-call(f32[32,128]{1,0:T(8,128)} %bitcast.16, s32[32,128]{1,0:T(8,128)} %bitcast.17, s32[32,128]{1,0:T(8,128)} %bitcast.18, s32[32,128]{1,0:T(8,128)} %bitcast.19, s32[32,128]{1,0:T(8,128)} %bitcast.20, ...), custom_call_target="tpu_custom_call" | custom-call | tf_op jit(solution)/shard_map/sort/pallas_call | solution.py:526
  3.1 3.8 %collective-permute-start = (f32[4,32,128]{2,1,0:T(8,128)S(1)}, f32[4,32,128]{2,1,0:T(8,128)S(1)}, u32[]{:S(2)}, u32[]{:S(2)}) collective-permute-start(f32[4,32,128]{2,1,0:T(8,128)S(1)} %get-tuple-element.17), channel_id=1, source_target_pairs={{0,64},{32,96},{64,0},{96,32},{1,65},{33,97},{65,1},{97,33},{2,66}... | collective-permute-start | bytes 196616 | tf_op jit(solution)/shard_map/ppermute | solution.py:623
  6.9 0.4 collective-permute-start.1
  7.3 2.3 %collective-permute-start.2 = (f32[4,32,128]{2,1,0:T(8,128)S(1)}, f32[4,32,128]{2,1,0:T(8,128)S(1)}, u32[]{:S(2)}, u32[]{:S(2)}) collective-permute-start(f32[4,32,128]{2,1,0:T(8,128)S(1)} %get-tuple-element.19), channel_id=1, source_target_pairs={{0,96},{32,0},{64,32},{96,64},{1,97},{33,1},{65,33},{97,65},{2,98}... | collective-permute-start | bytes 196616 | tf_op jit(solution)/shard_map/ppermute | solution.py:623
  9.6 1.1 %tables.1 = (bf16[2,512,512]{2,1,0:T(8,128)(2,1)S(1)}, bf16[2,128,256]{2,1,0:T(8,128)(2,1)S(1)}, f32[2,33,640]{2,1,0:T(8,128)S(1)}, f32[2,16,640]{2,1,0:T(8,128)S(1)}, f32[32,8,128]{2,1,0:T(8,128)S(1)}) custom-call(bf16[2,16,512]{2,1,0:T(8,128)(2,1)} %constant.18.clone.fm_h, bf16[2,128,256]{2,1,0:T(8,128)(2,1)} %constant.19.clone.fl_h, ...), custom_call_target="tpu_custom_call" | custom-call | tf_op jit(solution)/shard_map/tables/pallas_call | solution.py:550
  10.7 0.0 collective-permute-done.g1
  10.7 0.5 collective-permute-done.1.g2
  11.2 0.0 collective-permute-done.2.g3
  11.2 6.5 %spectra.1 = f32[1408,128]{1,0:T(8,128)} custom-call(f32[4,32,128]{2,1,0:T(8,128)S(1)} %get-tuple-element.16.g0, f32[4,32,128]{2,1,0:T(8,128)S(1)} %collective-permute-done.g1, f32[4,32,128]{2,1,0:T(8,128)S(1)} %collective-permute-done.1.g2, f32[4,32,128]{2,1,0:T(8,128)S(1)} %collective-permute-done.2.g3, bf16[2,512,512]{2,1,0:T(8,128)(2,1)S(1)} %get-tuple-element.20.s1_ref, ...), custom_call_target="tpu_custom_call" | custom-call | tf_op jit(solution)/shard_map/spectra/pallas_call | solution.py:566
  17.7 11.3 %all-to-all-start = ((f32[128,1,1408]{2,1,0:T(1,128)}), f32[128,1,1408]{2,1,0:T(1,128)S(1)}, u32[]{:S(2)}, u32[]{:S(2)}) async-start(f32[128,1,1408]{2,1,0:T(1,128)} %bitcast.7), calls=%async_computation | async-start | bytes 1441792 | tf_op jit(solution)/shard_map/all_to_all | solution.py:627
  29.1 1.6 %early.1 = (f32[2,2120,128]{2,1,0:T(8,128)S(1)}, bf16[2,80,80]{2,1,0:T(8,128)(2,1)S(1)}) custom-call(f32[20,2112,128]{2,1,0:T(8,128)} %bitcast.14, bf16[2,80,80]{2,1,0:T(8,128)(2,1)} %constant.23.clone.d_h), custom_call_target="tpu_custom_call" | custom-call | tf_op jit(solution)/shard_map/early/pallas_call | solution.py:586
  30.7 14.2 %all-to-all-done = f32[128,1,1408]{2,1,0:T(1,128)S(1)} async-done(((f32[128,1,1408]{2,1,0:T(1,128)}), f32[128,1,1408]{2,1,0:T(1,128)S(1)}, u32[]{:S(2)}, u32[]{:S(2)}) %all-to-all-start) | async-done | bytes 720928 | tf_op jit(solution)/shard_map/all_to_all | solution.py:627
  44.9 0.0 copy-done
  44.9 8.1 %sky.1 = f32[20,1,128]{2,1,0:T(1,128)} custom-call(f32[1408,128]{1,0:T(8,128)S(1)} %bitcast.12, f32[20,2112,128]{2,1,0:T(8,128)} %bitcast.15, f32[2,2120,128]{2,1,0:T(8,128)S(1)} %get-tuple-element.25.head_ref, f32[33,64]{1,0:T(8,128)S(1)} %bitcast.13, bf16[2,80,80]{2,1,0:T(8,128)(2,1)S(1)} %get-tuple-element.26.d_ref), custom_call_target="tpu_custom_call" | custom-call | tf_op jit(solution)/shard_map/sky/pallas_call | solution.py:598
Async XLA Ops:
  0.0 44.9 %copy-start = (f32[64,33]{0,1:T(8,128)S(1)}, f32[64,33]{0,1:T(8,128)}, u32[]{:S(2)}) copy-start(f32[64,33]{0,1:T(8,128)} %param.23) | copy-start | bytes 25348
  3.1 7.6 %collective-permute-start = (f32[4,32,128]{2,1,0:T(8,128)S(1)}, f32[4,32,128]{2,1,0:T(8,128)S(1)}, u32[]{:S(2)}, u32[]{:S(2)}) collective-permute-start(f32[4,32,128]{2,1,0:T(8,128)S(1)} %get-tuple-element.17), channel_id=1, source_target_pairs={{0,64},{32,96},{64,0},{96,32},{1,65},{33,97},{65,1},{97,33},{2,66}... | collective-permute-start | bytes 196616 | tf_op jit(solution)/shard_map/ppermute | solution.py:623
  6.9 4.3 %collective-permute-start.1 = (f32[4,32,128]{2,1,0:T(8,128)S(1)}, f32[4,32,128]{2,1,0:T(8,128)S(1)}, u32[]{:S(2)}, u32[]{:S(2)}) collective-permute-start(f32[4,32,128]{2,1,0:T(8,128)S(1)} %get-tuple-element.18), channel_id=1, source_target_pairs={{0,32},{32,64},{64,96},{96,0},{1,33},{33,65},{65,97},{97,1},{2,34}... | collective-permute-start | bytes 196616 | tf_op jit(solution)/shard_map/ppermute | solution.py:623
  7.3 3.9 %collective-permute-start.2 = (f32[4,32,128]{2,1,0:T(8,128)S(1)}, f32[4,32,128]{2,1,0:T(8,128)S(1)}, u32[]{:S(2)}, u32[]{:S(2)}) collective-permute-start(f32[4,32,128]{2,1,0:T(8,128)S(1)} %get-tuple-element.19), channel_id=1, source_target_pairs={{0,96},{32,0},{64,32},{96,64},{1,97},{33,1},{65,33},{97,65},{2,98}... | collective-permute-start | bytes 196616 | tf_op jit(solution)/shard_map/ppermute | solution.py:623
  17.7 27.2 %all-to-all-start = ((f32[128,1,1408]{2,1,0:T(1,128)}), f32[128,1,1408]{2,1,0:T(1,128)S(1)}, u32[]{:S(2)}, u32[]{:S(2)}) async-start(f32[128,1,1408]{2,1,0:T(1,128)} %bitcast.7), calls=%async_computation | async-start | bytes 1441792 | tf_op jit(solution)/shard_map/all_to_all | solution.py:627

commit v5 on v4

--- a/solution.py
+++ b/solution.py
@@ -194,43 +194,14 @@
         out_ref[3] = jnp.where(valid, take(6), 0.0)
 
 
-def tables_kernel(
-    fm_h, fl_h, th_h, tl_h, kern_h, s1_ref, fl_ref, th_ref, tl_ref, kb_ref, fm_ref, kern_ref, sems
-):
-    pairs = (
-        (fm_h, fm_ref), (fl_h, fl_ref), (th_h, th_ref), (tl_h, tl_ref), (kern_h, kern_ref)
-    )
-    copies = [pltpu.make_async_copy(a, b, sems.at[i]) for i, (a, b) in enumerate(pairs)]
-    for c in copies:
-        c.start()
-    copies[0].wait()
-    lane = lax.broadcasted_iota(jnp.int32, (16, 512), 1) & 31
-    lane = lane.astype(jnp.float32).astype(BF)
-    for q in range(32):
-        keep = lane == float(q)
-        for part in range(2):
-            s1_ref[part, q * 16 : (q + 1) * 16, :] = jnp.where(
-                keep, fm_ref[part], jnp.zeros((16, 512), BF)
-            )
-    for c in copies[1:]:
-        c.wait()
-    for t in range(4):
-        for o in range(8):
-            kb_ref[t * 8 + o] = jnp.full((8, 128), kern_ref[t, o], jnp.float32)
-
-
-def spectra_kernel(
-    g0, g1, g2, g3, s1_ref, fl_ref, th_ref, tl_ref, kb_ref, w_h, out_ref,
-    s_ref, acc_ref, last_ref, zh_ref, zl_ref, w_ref, w_sem,
-):
-    w_copy = pltpu.make_async_copy(w_h, w_ref, w_sem.at[0])
-    w_copy.start()
+def prepare(lists, kb_ref, s_ref):
+    spare = len(lists) * ROWS
     ends, skips = [], []
     total = jnp.int32(0)
-    s_ref[0, 4 * ROWS : 4 * ROWS + 8, :] = jnp.full((8, 128), -1.0, jnp.float32)
+    s_ref[0, spare : spare + 8, :] = jnp.full((8, 128), -1.0, jnp.float32)
     for ch in range(1, 8):
-        s_ref[ch, 4 * ROWS : 4 * ROWS + 8, :] = jnp.zeros((8, 128), jnp.float32)
-    for s, g_ref in enumerate((g0, g1, g2, g3)):
+        s_ref[ch, spare : spare + 8, :] = jnp.zeros((8, 128), jnp.float32)
+    for s, g_ref in enumerate(lists):
         tod = g_ref[0]
         phi = g_ref[1].astype(jnp.int32)
         psi = g_ref[2].astype(jnp.int32)
@@ -255,8 +226,11 @@
                 entry = jnp.concatenate([kb_ref[t * 8 + o]] * (ROWS // 8), 0)
                 weight = jnp.where(off == o, entry, weight)
             s_ref[4 + t, at, :] = (tod * weight).astype(BF).astype(jnp.float32)
-
-    acc_ref[...] = jnp.zeros_like(acc_ref)
+    return ends, skips, total
+
+
+def deposit(s_ref, acc_ref, ends, skips, total):
+    spare = len(ends) * ROWS
     sub = lax.broadcasted_iota(jnp.int32, (16, 128), 0).astype(jnp.float32).astype(BF)
     zero = jnp.zeros((16, 128), BF)
     one = jnp.ones((16, 128), BF)
@@ -266,9 +240,9 @@
         for j in range(BLOCK):
             f = first + j
             r = f
-            for s in range(4):
+            for s in range(len(ends)):
                 r = r + jnp.where(f >= ends[s], skips[s], 0)
-            r = jnp.minimum(r, 4 * ROWS)
+            r = jnp.minimum(r, spare)
 
             def row(ch):
                 v = s_ref[ch, pl.ds(r, 1), :]
@@ -300,16 +274,55 @@
 
     def step(i, carry):
         left, right = build(i * BLOCK)
-        total = None
+        sums = None
         for j in range(0, BLOCK, 2):
             part = dot_nt(
                 jnp.concatenate(right[j : j + 2], 1), jnp.concatenate(left[j : j + 2], 1)
             )
-            total = part if total is None else total + part
-        acc_ref[...] += total
+            sums = part if sums is None else sums + part
+        acc_ref[...] += sums
         return carry
 
     lax.fori_loop(0, (total + BLOCK - 1) // BLOCK, step, 0)
+
+
+def tables_kernel(
+    g_ref, fm_h, fl_h, th_h, tl_h, kern_h, s1_ref, fl_ref, th_ref, tl_ref, kb_ref, acc_ref,
+    fm_ref, kern_ref, s_ref, sems,
+):
+    pairs = (
+        (fm_h, fm_ref), (fl_h, fl_ref), (th_h, th_ref), (tl_h, tl_ref), (kern_h, kern_ref)
+    )
+    copies = [pltpu.make_async_copy(a, b, sems.at[i]) for i, (a, b) in enumerate(pairs)]
+    for c in copies:
+        c.start()
+    copies[4].wait()
+    for t in range(4):
+        for o in range(8):
+            kb_ref[t * 8 + o] = jnp.full((8, 128), kern_ref[t, o], jnp.float32)
+    acc_ref[...] = jnp.zeros_like(acc_ref)
+    deposit(s_ref, acc_ref, *prepare((g_ref,), kb_ref, s_ref))
+    copies[0].wait()
+    lane = lax.broadcasted_iota(jnp.int32, (16, 512), 1) & 31
+    lane = lane.astype(jnp.float32).astype(BF)
+    for q in range(32):
+        keep = lane == float(q)
+        for part in range(2):
+            s1_ref[part, q * 16 : (q + 1) * 16, :] = jnp.where(
+                keep, fm_ref[part], jnp.zeros((16, 512), BF)
+            )
+    for c in copies[1:4]:
+        c.wait()
+
+
+def spectra_kernel(
+    g1, g2, g3, s1_ref, fl_ref, th_ref, tl_ref, kb_ref, own_ref, w_h, out_ref,
+    s_ref, acc_ref, last_ref, zh_ref, zl_ref, w_ref, w_sem,
+):
+    w_copy = pltpu.make_async_copy(w_h, w_ref, w_sem.at[0])
+    w_copy.start()
+    acc_ref[...] = own_ref[...]
+    deposit(s_ref, acc_ref, *prepare((g1, g2, g3), kb_ref, s_ref))
 
     def chunk(r0, at):
         tile = acc_ref[r0 : r0 + 16, (at // 8) * 128 : (at // 8) * 128 + 128]
@@ -544,22 +557,23 @@
     )(*stay(tod, cycle, phi_cell, psi_bin, offset), counts, mine)
 
 
-def tables(kernel):
-    shapes = ((2, 512, 512), F_LAST.shape, TW_HI.shape, TW_LO.shape, (32, 8, 128))
-    types = (BF, BF) + (jnp.float32,) * 3
+def tables(own, kernel):
+    shapes = ((2, 512, 512), F_LAST.shape, TW_HI.shape, TW_LO.shape, (32, 8, 128), (CELL_ROWS, 512))
+    types = (BF, BF) + (jnp.float32,) * 4
     return pl.pallas_call(
         tables_kernel,
         out_shape=[pltpu.VMEM(s, t) for s, t in zip(shapes, types)],
-        in_specs=[hbm()] * 5,
-        out_specs=[vmem()] * 5,
+        in_specs=[vmem()] + [hbm()] * 5,
+        out_specs=[vmem()] * 6,
         scratch_shapes=[
             pltpu.VMEM((2, 16, 512), BF),
             pltpu.SMEM((4, 8), jnp.float32),
+            pltpu.VMEM((8, ROWS + 8, 128), jnp.float32),
             pltpu.SemaphoreType.DMA((5,)),
         ],
-        compiler_params=pltpu.CompilerParams(vmem_limit_bytes=8 << 20),
+        compiler_params=pltpu.CompilerParams(vmem_limit_bytes=16 << 20),
         name="tables",
-    )(*stay(F_MAIN, F_LAST, TW_HI, TW_LO, kernel))
+    )(own, *stay(F_MAIN, F_LAST, TW_HI, TW_LO, kernel))
 
 
 def spectra(lists, *consts):
@@ -569,7 +583,7 @@
         in_specs=[vmem()] * 9 + [hbm()],
         out_specs=vmem(),
         scratch_shapes=[
-            pltpu.VMEM((8, 4 * ROWS + 8, 128), jnp.float32),
+            pltpu.VMEM((8, 3 * ROWS + 8, 128), jnp.float32),
             pltpu.VMEM((CELL_ROWS, 512), jnp.float32),
             pltpu.VMEM((528, 128), jnp.float32),
             pltpu.VMEM((2, 256, 1280), BF),
@@ -619,11 +633,11 @@
     flat = [x.reshape(ROWS, 128) for x in (tod, cycle, phi_cell, psi_bin, offset)]
     mine = lax.axis_index("samp").astype(jnp.int32).reshape(1)
     lists = sort(*flat, counts, mine)
-    gathered = [lists[0]] + [
+    moved = [
         lax.ppermute(lists[d], "samp", [(i, (i + d) % 4) for i in range(4)]) for d in (2, 1, 3)
     ]
-    consts = tables(kernel.T)
-    sent = spectra(gathered, *consts)
+    consts = tables(lists[0], kernel.T)
+    sent = spectra(moved, *consts)
     received = lax.all_to_all(sent.reshape(128, 1, TILES * 128), ("band", "samp"), 0, 0, tiled=True)
     wigner = wigner.reshape(PER_DEV, WROWS, RT)
     head, d = early(wigner)

time: 53.4 us -> 53.3 us (level)
  Pallas kernels: 19.8 us -> 20.5 us
    pallas_call x1, Pallas kernels: 1.13 us -> 1.94 us  [tables(): pl.pallas_call(tables_kernel, out_shape=[pltpu.VMEM(s, t) for s, t in zip...]
  transfers between devices with their start and end apart: 4 -> 4, of which waited for: 2 -> 1; matrix products, arithmetic and copies ran while one was open for 0% -> 0% of each run, Pallas kernels for 5% -> 7%
where the time goes in v5:
time: 53.3 us; the launch traced here: 53 us
  Pallas kernels  20.5 us (38%)
  starting transfers between devices  17.5 us (33%)
  waiting for transfers between devices  14.2 us (27%)
  between operations  0.73 us (1%)
    all_to_all x1, waiting for transfers between devices, body(): lax.all_to_all(sent.reshape(128, 1, TILES * 128), ('band', 'samp'), 0, 0,...  14.2 us
    all_to_all x1, starting transfers between devices, body(): lax.all_to_all(sent.reshape(128, 1, TILES * 128), ('band', 'samp'), 0, 0,...  11 us
    pallas_call x1, Pallas kernels, sky_of(): pl.pallas_call(sky_kernel, out_shape=pltpu.HBM((PER_DEV, 1, 2 * LB), jnp....  8.15 us
    ppermute x3, starting transfers between devices, body(): lax.ppermute(lists[d], 'samp', [(i, (i + d) % 4) for i in range(4)])  6.49 us
    pallas_call x1, Pallas kernels, spectra(): pl.pallas_call(spectra_kernel, out_shape=jax.ShapeDtypeStruct((128 * TILE...  6.44 us
    pallas_call x1, Pallas kernels, sort(): pl.pallas_call(sort_kernel, out_shape=[jax.ShapeDtypeStruct((4, ROWS, 128...  2.4 us
    pallas_call x1, Pallas kernels, tables(): pl.pallas_call(tables_kernel, out_shape=[pltpu.VMEM(s, t) for s, t in zip...  1.94 us
    pallas_call x1, Pallas kernels, early(): pl.pallas_call(early_kernel, out_shape=[pltpu.VMEM((HEAD, WPAD, RT), jnp....  1.62 us
  transfers between devices with their start and end apart: 4, of which 1 were waited for; matrix products, arithmetic and copies ran while one was open for 0% of the time, Pallas kernels for 7%

profile of v5, /device:TPU:1, one launch (start us, length us, event | category | flops | bytes accessed | tf_op | source)
XLA Modules:
  0.0 53.0 jit_solution(2618613986188021269)
XLA Ops:
  0.7 2.4 %sort.1 = (f32[4,32,128]{2,1,0:T(8,128)S(1)}, f32[4,32,128]{2,1,0:T(8,128)S(1)}, f32[4,32,128]{2,1,0:T(8,128)S(1)}, f32[4,32,128]{2,1,0:T(8,128)S(1)}) custom-call(f32[32,128]{1,0:T(8,128)} %bitcast.16, s32[32,128]{1,0:T(8,128)} %bitcast.17, s32[32,128]{1,0:T(8,128)} %bitcast.18, s32[32,128]{1,0:T(8,128)} %bitcast.19, s32[32,128]{1,0:T(8,128)} %bitcast.20, ...), custom_call_target="tpu_custom_call" | custom-call | tf_op jit(solution)/shard_map/sort/pallas_call | solution.py:539
  3.1 3.8 %collective-permute-start = (f32[4,32,128]{2,1,0:T(8,128)S(1)}, f32[4,32,128]{2,1,0:T(8,128)S(1)}, u32[]{:S(2)}, u32[]{:S(2)}) collective-permute-start(f32[4,32,128]{2,1,0:T(8,128)S(1)} %get-tuple-element.17), channel_id=1, source_target_pairs={{0,64},{32,96},{64,0},{96,32},{1,65},{33,97},{65,1},{97,33},{2,66}... | collective-permute-start | bytes 196616 | tf_op jit(solution)/shard_map/ppermute | solution.py:637
  6.9 0.4 collective-permute-start.1
  7.3 2.3 %collective-permute-start.2 = (f32[4,32,128]{2,1,0:T(8,128)S(1)}, f32[4,32,128]{2,1,0:T(8,128)S(1)}, u32[]{:S(2)}, u32[]{:S(2)}) collective-permute-start(f32[4,32,128]{2,1,0:T(8,128)S(1)} %get-tuple-element.19), channel_id=1, source_target_pairs={{0,96},{32,0},{64,32},{96,64},{1,97},{33,1},{65,33},{97,65},{2,98}... | collective-permute-start | bytes 196616 | tf_op jit(solution)/shard_map/ppermute | solution.py:637
  9.6 1.9 %tables.1 = (bf16[2,512,512]{2,1,0:T(8,128)(2,1)S(1)}, bf16[2,128,256]{2,1,0:T(8,128)(2,1)S(1)}, f32[2,33,640]{2,1,0:T(8,128)S(1)}, f32[2,16,640]{2,1,0:T(8,128)...) custom-call(f32[4,32,128]{2,1,0:T(8,128)S(1)} %get-tuple-element.20.g_ref, ...), custom_call_target="tpu_custom_call" | custom-call | tf_op jit(solution)/shard_map/tables/pallas_call | solution.py:563
  11.5 0.0 collective-permute-done.g1
  11.5 0.0 collective-permute-done.1.g2
  11.5 0.0 collective-permute-done.2.g3
  11.5 6.4 %spectra.1 = f32[1408,128]{1,0:T(8,128)} custom-call(f32[4,32,128]{2,1,0:T(8,128)S(1)} %collective-permute-done.g1, f32[4,32,128]{2,1,0:T(8,128)S(1)} %collective-permute-done.1.g2, f32[4,32,128]{2,1,0:T(8,128)S(1)} %collective-permute-done.2.g3, bf16[2,512,512]{2,1,0:T(8,128)(2,1)S(1)} %get-tuple-element.21.s1_ref, ...), custom_call_target="tpu_custom_call" | custom-call | tf_op jit(solution)/shard_map/spectra/pallas_call | solution.py:580
  18.0 11.0 %all-to-all-start = ((f32[128,1,1408]{2,1,0:T(1,128)}), f32[128,1,1408]{2,1,0:T(1,128)S(1)}, u32[]{:S(2)}, u32[]{:S(2)}) async-start(f32[128,1,1408]{2,1,0:T(1,128)} %bitcast.7), calls=%async_computation | async-start | bytes 1441792 | tf_op jit(solution)/shard_map/all_to_all | solution.py:641
  29.0 0.0 copy-start
  29.0 1.6 %early.1 = (f32[2,2120,128]{2,1,0:T(8,128)S(1)}, bf16[2,80,80]{2,1,0:T(8,128)(2,1)S(1)}) custom-call(f32[20,2112,128]{2,1,0:T(8,128)} %bitcast.14, bf16[2,80,80]{2,1,0:T(8,128)(2,1)} %constant.23.clone.d_h), custom_call_target="tpu_custom_call" | custom-call | tf_op jit(solution)/shard_map/early/pallas_call | solution.py:600
  30.6 14.2 %all-to-all-done = f32[128,1,1408]{2,1,0:T(1,128)S(1)} async-done(((f32[128,1,1408]{2,1,0:T(1,128)}), f32[128,1,1408]{2,1,0:T(1,128)S(1)}, u32[]{:S(2)}, u32[]{:S(2)}) %all-to-all-start) | async-done | bytes 720928 | tf_op jit(solution)/shard_map/all_to_all | solution.py:641
  44.8 0.0 copy-done
  44.8 8.1 %sky.1 = f32[20,1,128]{2,1,0:T(1,128)} custom-call(f32[1408,128]{1,0:T(8,128)S(1)} %bitcast.12, f32[20,2112,128]{2,1,0:T(8,128)} %bitcast.15, f32[2,2120,128]{2,1,0:T(8,128)S(1)} %get-tuple-element.27.head_ref, f32[33,64]{1,0:T(8,128)S(1)} %bitcast.13, bf16[2,80,80]{2,1,0:T(8,128)(2,1)S(1)} %get-tuple-element.28.d_ref), custom_call_target="tpu_custom_call" | custom-call | tf_op jit(solution)/shard_map/sky/pallas_call | solution.py:612
Async XLA Ops:
  3.1 8.4 %collective-permute-start = (f32[4,32,128]{2,1,0:T(8,128)S(1)}, f32[4,32,128]{2,1,0:T(8,128)S(1)}, u32[]{:S(2)}, u32[]{:S(2)}) collective-permute-start(f32[4,32,128]{2,1,0:T(8,128)S(1)} %get-tuple-element.17), channel_id=1, source_target_pairs={{0,64},{32,96},{64,0},{96,32},{1,65},{33,97},{65,1},{97,33},{2,66}... | collective-permute-start | bytes 196616 | tf_op jit(solution)/shard_map/ppermute | solution.py:637
  6.9 4.6 %collective-permute-start.1 = (f32[4,32,128]{2,1,0:T(8,128)S(1)}, f32[4,32,128]{2,1,0:T(8,128)S(1)}, u32[]{:S(2)}, u32[]{:S(2)}) collective-permute-start(f32[4,32,128]{2,1,0:T(8,128)S(1)} %get-tuple-element.18), channel_id=1, source_target_pairs={{0,32},{32,64},{64,96},{96,0},{1,33},{33,65},{65,97},{97,1},{2,34}... | collective-permute-start | bytes 196616 | tf_op jit(solution)/shard_map/ppermute | solution.py:637
  7.3 4.2 %collective-permute-start.2 = (f32[4,32,128]{2,1,0:T(8,128)S(1)}, f32[4,32,128]{2,1,0:T(8,128)S(1)}, u32[]{:S(2)}, u32[]{:S(2)}) collective-permute-start(f32[4,32,128]{2,1,0:T(8,128)S(1)} %get-tuple-element.19), channel_id=1, source_target_pairs={{0,96},{32,0},{64,32},{96,64},{1,97},{33,1},{65,33},{97,65},{2,98}... | collective-permute-start | bytes 196616 | tf_op jit(solution)/shard_map/ppermute | solution.py:637
  18.0 26.9 %all-to-all-start = ((f32[128,1,1408]{2,1,0:T(1,128)}), f32[128,1,1408]{2,1,0:T(1,128)S(1)}, u32[]{:S(2)}, u32[]{:S(2)}) async-start(f32[128,1,1408]{2,1,0:T(1,128)} %bitcast.7), calls=%async_computation | async-start | bytes 1441792 | tf_op jit(solution)/shard_map/all_to_all | solution.py:641
  29.0 15.8 %copy-start = (f32[64,33]{0,1:T(8,128)S(1)}, f32[64,33]{0,1:T(8,128)}, u32[]{:S(2)}) copy-start(f32[64,33]{0,1:T(8,128)} %param.23) | copy-start | bytes 25348
